TPU v7x, 256 devices: a 2x2x32 block of a 4x8x32 slice. The times are simulated.
256 devices in a mesh: groups: 4 (over x, y), tp: 32 (over z), role: 2 (over core).
Axes of the slice: x: 2, y: 2, z: 32, core: 2. Of those that a mesh axis runs over, the one named last changes fastest.
The devices are a block of a 4x8x32 slice.
Arguments:
- rows_in: bfloat16 [2, 2048, 8192], P('role', 'groups', 'tp'), parts along dimension 1, may hold values from -6 to 6
- norm_gain: bfloat16 [8192], replicated, may hold values from 0.5 to 4
- q_words: int32 [1024, 8192], P(None, 'tp'), may hold values from -2147483648 to 2147483646
- q_scales: bfloat16 [64, 8192], P(None, 'tp'), may hold values from 0.0011978149 to 0.0047912598
- kv_words: int32 [32, 1024, 256], P('tp'), may hold values from -2147483648 to 2147483646, as said below
- kv_scales: bfloat16 [32, 64, 256], P('tp'), may hold values from 0.0012 to 0.0048, as said below
- o_words: int32 [1024, 8192], P('tp'), may hold values from -2147483648 to 2147483646
- o_scales: bfloat16 [64, 8192], P('tp'), may hold values from 0.0011978149 to 0.0047912598
- kv_pool: bfloat16 [32, 4096, 16, 256], P('tp', 'groups'), parts along dimension 1, may hold values from -120 to 120, as said below
- prompt_pages: int32 [64], P('groups'), parts along dimension 0, may hold values from 1 to 8, 32 in all
- page_slots: int32 [128], P('groups'), parts along dimension 0, may hold values from 0 to 1023, as said below
- block_tables: int32 [1984, 16], P('groups'), parts along dimension 0, may hold values from 0 to 1023, as said below
- cache_lens: int32 [1984], P('groups'), parts along dimension 0, may hold values from 1 to 256
Outputs:
- layer_out: bfloat16 [2, 2048, 8192], P('role', 'groups', 'tp'), parts along dimension 1
There are 4 independent parts, one for each index of `groups`. A program takes and returns all parts, laid end to end along the dimension named above; an argument that names none is the same for every part. Nothing has to cross between parts.
Inputs may be any that keep to these rules, and one draw needn't show every extreme that they name: `kv_words`: entries t and u are equal whenever t * 8 // 32 equals u * 8 // 32. `kv_scales`: entries t and u are equal whenever t * 8 // 32 equals u * 8 // 32. `kv_pool`: entries t and u are equal whenever t * 8 // 32 equals u * 8 // 32. `page_slots`: distinct pages; entry j receives the j-th page of the prompts taken in order. `block_tables`: no entry is one of page_slots; sequences may share pages.
All inputs are finite; a program needn't handle non-finite values.
Results may differ from a plain program's by a relative error of at most 0.015.
The roundings to bfloat16 on the way count: a program that leaves them out, or rounds other values in their place, can miss the bound.
Values may be sent and summed in bfloat16 or wider, within the bound.
A program may use at most 192 MiB of HBM per device.

v0:
```python
import jax
import jax.numpy as jnp
from jax import lax
from jax.sharding import PartitionSpec as P

HD = 128


def passed_along(block, axis, distance):
    devices = range(lax.axis_size(axis))
    route = [(i - distance, i) for i in devices if i - distance in devices]
    return lax.ppermute(block, axis, route)


def unpack_words(words, scales):
    shifts = jnp.arange(8, dtype=jnp.int32) * 4
    nibbles = jnp.bitwise_and(jnp.right_shift(words[:, None, :], shifts[None, :, None]), 15) - 8
    values = nibbles.reshape(words.shape[0] * 8, words.shape[1]).astype(jnp.float32)
    group = values.shape[0] // scales.shape[0]
    spread = jnp.repeat(scales.astype(jnp.float32), group, axis=0)
    return (values * spread).astype(jnp.bfloat16)


def rms_normed(rows, gain):
    wide = rows.astype(jnp.float32)
    inverse = lax.rsqrt(jnp.mean(wide * wide, axis=-1, keepdims=True) + 1e-05)
    return (wide * inverse * gain.astype(jnp.float32)).astype(jnp.bfloat16)


def rotate(heads, positions):
    half = heads.shape[-1] // 2
    freq = 500000.0 ** (-jnp.arange(half, dtype=jnp.float32) * 2.0 / heads.shape[-1])
    angle = positions.astype(jnp.float32)[:, None, None] * freq[None, None, :]
    cosine = jnp.cos(angle)
    sine = jnp.sin(angle)
    first = heads[..., :half]
    second = heads[..., half:]
    return jnp.concatenate(
        [first * cosine - second * sine, second * cosine + first * sine], axis=-1
    )


def layout(prompt_pages, page_slots, block_tables, cache_lens, rows):
    page = rows // page_slots.shape[0]
    count = prompt_pages.shape[0]
    ends = jnp.cumsum(prompt_pages) * page
    starts = ends - prompt_pages * page
    index = jnp.arange(rows, dtype=jnp.int32)
    member = (index[:, None] >= starts[None, :]) & (index[:, None] < ends[None, :])
    doc = jnp.sum(jnp.where(member, jnp.arange(count, dtype=jnp.int32)[None, :], 0), axis=1)
    prefill_pos = index - jnp.sum(jnp.where(member, starts[None, :], 0), axis=1)
    span = block_tables.shape[1]
    picks = jnp.minimum(
        starts[:, None] // page + jnp.arange(span, dtype=jnp.int32)[None, :],
        page_slots.shape[0] - 1,
    )
    prompt_table = page_slots[picks]
    table = jnp.concatenate([prompt_table, block_tables], axis=0)
    lengths = jnp.concatenate([prompt_pages * page, cache_lens])
    return (doc, prefill_pos, table, lengths)


def prefill_attend(query, keys, values, doc):
    rows = query.shape[0]
    block = min(512, rows)
    score_scale = query.shape[-1] ** (-0.5)
    index = jnp.arange(rows, dtype=jnp.int32)

    def prefill_one_block(start):
        logit_scores = (
            jnp.einsum("qhd,kd->hqk", query, keys, preferred_element_type=jnp.float32) * score_scale
        )
        own = start + jnp.arange(block, dtype=jnp.int32)
        allowed = (doc[:, None] == doc[None, :]) & (index[None, :] <= own[:, None])
        logit_scores = jnp.where(allowed[None], logit_scores, -1e30)
        attention_probs = jax.nn.softmax(logit_scores, axis=-1).astype(jnp.bfloat16)
        return jnp.einsum(
            "hqk,kd->qhd", attention_probs, values, preferred_element_type=jnp.float32
        ).astype(jnp.bfloat16)

    starts = jnp.arange(0, rows, block, dtype=jnp.int32)
    done = lax.map(prefill_one_block, starts)
    return done.reshape(rows, query.shape[1], query.shape[2])


def decode_attend(query, key_self, value_self, cache, table, lengths):
    rows = query.shape[0]
    block = min(128, rows)
    score_scale = query.shape[-1] ** (-0.5)
    head_dim = query.shape[-1]

    def decode_one_block(start):
        partial_query = lax.dynamic_slice_in_dim(query, start, block, 0)
        part_table = lax.dynamic_slice_in_dim(table, start, block, 0)
        part_len = lax.dynamic_slice_in_dim(lengths, start, block, 0)
        pages = cache[part_table]
        pages = pages.reshape(block, pages.shape[1] * pages.shape[2], pages.shape[3])
        own_key = lax.dynamic_slice_in_dim(key_self, start, block, 0)
        own_value = lax.dynamic_slice_in_dim(value_self, start, block, 0)
        gathered_keys = jnp.concatenate([pages[..., :head_dim], own_key[:, None, :]], axis=1)
        gathered_values = jnp.concatenate([pages[..., head_dim:], own_value[:, None, :]], axis=1)
        logit_scores = (
            jnp.einsum(
                "jai,jri->jar", partial_query, gathered_keys, preferred_element_type=jnp.float32
            )
            * score_scale
        )
        spots = jnp.arange(pages.shape[1], dtype=jnp.int32)
        valid = jnp.concatenate(
            [spots[None, :] < part_len[:, None], jnp.ones((block, 1), dtype=bool)], axis=1
        )
        logit_scores = jnp.where(valid[:, None, :], logit_scores, -1e30)
        attention_probs = jax.nn.softmax(logit_scores, axis=-1).astype(jnp.bfloat16)
        return jnp.einsum(
            "cwt,ctr->cwr", attention_probs, gathered_values, preferred_element_type=jnp.float32
        ).astype(jnp.bfloat16)

    starts = jnp.arange(0, rows, block, dtype=jnp.int32)
    done = lax.map(decode_one_block, starts)
    return done.reshape(rows, query.shape[1], query.shape[2])


def local(
    rows_in,
    norm_gain,
    q_words,
    q_scales,
    kv_words,
    kv_scales,
    o_words,
    o_scales,
    kv_pool,
    prompt_pages,
    page_slots,
    block_tables,
    cache_lens,
):
    side = lax.axis_index("role")
    whole = lax.all_gather(rows_in[0], "tp", axis=1, tiled=True)
    rows = whole.shape[0]
    normed = rms_normed(whole, norm_gain)
    doc, prefill_pos, table, lengths = layout(
        prompt_pages, page_slots, block_tables, cache_lens, rows
    )
    positions = jnp.where(side == 0, prefill_pos, lengths)
    w_query = unpack_words(q_words, q_scales)
    w_keyval = unpack_words(kv_words[0], kv_scales[0])
    projected = jnp.dot(normed, w_query, preferred_element_type=jnp.float32)
    query = rotate(projected.reshape(rows, -1, HD), positions).astype(jnp.bfloat16)
    keyval = jnp.dot(normed, w_keyval, preferred_element_type=jnp.float32)
    key_new = rotate(keyval[:, None, :HD], positions)[:, 0].astype(jnp.bfloat16)
    value_new = keyval[:, HD:].astype(jnp.bfloat16)
    fresh = jnp.concatenate([key_new, value_new], axis=1)
    arrived = passed_along(fresh, "role", 1)
    pool = kv_pool[0]

    def run_prefill():
        return prefill_attend(query, key_new, value_new, doc)

    def run_decode():
        cache = pool.at[page_slots].set(arrived.reshape(-1, pool.shape[1], pool.shape[2]))
        return decode_attend(query, key_new, value_new, cache, table, lengths)

    attention_output = lax.cond(side == 0, run_prefill, run_decode).reshape(rows, -1)
    w_out = unpack_words(o_words, o_scales)
    partial_value = jnp.dot(attention_output, w_out, preferred_element_type=jnp.float32)
    summed = lax.psum_scatter(
        partial_value.astype(jnp.bfloat16), "tp", scatter_dimension=1, tiled=True
    )
    return summed[None]


def solution(mesh):
    return jax.shard_map(
        local,
        mesh=mesh,
        in_specs=(
            P("role", "groups", "tp"),
            P(),
            P(None, "tp"),
            P(None, "tp"),
            P("tp", None, None),
            P("tp", None, None),
            P("tp", None),
            P("tp", None),
            P("tp", "groups", None, None),
            P("groups"),
            P("groups"),
            P("groups", None),
            P("groups"),
        ),
        out_specs=P("role", "groups", "tp"),
        check_vma=False,
    )
```

profile of v0, /device:TPU:38, one launch (start us, length us, event | category | flops | bytes accessed | tf_op | source)
XLA Modules:
  0.0 580.4 jit_solution(14394088150767205824)
XLA Ops:
  6.6 7.3 %copy.97 = bf16[1,1024,16,256]{3,2,1,0:T(8,128)(2,1)} copy(bf16[1,1024,16,256]{3,2,1,0:T(8,128)(2,1)} %param.25) | data formatting | bytes 16777216
  14.1 0.1 copy.47
  14.2 0.3 shift_right_arithmetic.67
  14.6 6.5 %fusion.61 = (bf16[8192,256]{1,0:T(8,128)(2,1)}, bf16[8192,256]{1,0:T(8,128)(2,1)}) fusion(f32[64,256]{1,0:T(8,128)S(1)} %convert_element_type.89, s32[1024,256]{1,0:T(8,128)S(1)} %copy-done.4, s32[8192]{0:T(1024)S(1)} %shift_right_arithmetic.67, f32[64,256]{1,0:T(8,128)S(1)} %bitcast_convert_fusion.1, s32[1024,256]{1,0:T(8,128)S(1)} %bitcast.134), kind=kLoop, calls=%fused_computation.68 | loop fusion | flops 25165824 | bytes 10649600 | tf_op jit(solution)/shard_map/convert_element_type | solution.py:21
  21.1 6.5 %copy.64 = bf16[256,8192]{1,0:T(8,128)(2,1)} copy(bf16[256,8192]{0,1:T(8,128)(2,1)} %bitcast.129) | data formatting | bytes 8388608 | tf_op jit(solution)/shard_map/dot_general | solution.py:148
  27.5 0.1 multiply_reduce_fusion
  27.7 0.1 compare_select_fusion.2
  27.7 0.1 reshape.337
  27.8 1.9 gather_fusion.1
  29.7 0.1 reshape.336
  29.9 0.1 shift_right_arithmetic.76
  30.0 0.1 pad_add_fusion
  30.1 0.1 select_reduce_fusion.1
  30.2 0.1 select_convert_fusion
  30.3 0.1 fusion.82
  30.4 0.5 multiply_cosine_fusion
  30.9 0.9 shift_right_arithmetic.73
  31.9 3.5 fusion.60
  35.3 174.8 %all-gather.3.cloned.1.call-done = bf16[1,512,8192]{2,1,0:T(8,128)(2,1)} async-done(((bf16[1,512,256]{2,1,0:T(8,128)(2,1)}), bf16[1,512,8192]{2,1,0:T(8,128)(2,1)}) %all-gather.3.cloned.1.call-update) | async-done | bytes 8388624 | tf_op jit(solution)/shard_map/all_gather | solution.py:139
  210.2 5.3 fusion.53
  215.4 0.5 copy-done.1
  215.9 5.2 fusion.72
  221.2 0.6 fusion.79
  221.8 1.5 collective-permute-start
  223.3 2.6 fusion.65
  225.9 0.1 subtract_convert_fusion
  226.1 2.5 conditional.1
  226.1 0.2 fusion.5
  226.3 0.9 fusion.85
  227.3 1.3 fusion.2
  228.6 6.7 %bitcast_convert_fusion = bf16[512,8192]{1,0:T(8,128)(2,1)} fusion(bf16[512,2,128]{2,0,1:T(8,128)(2,1)S(1)} %get-tuple-element.305, bf16[2,128,8192]{2,1,0:T(8,128)(2,1)} %fusion.60), kind=kOutput, calls=%fused_computation.60 | convolution fusion | flops 2151677952 | bytes 12845056 | tf_op jit(solution)/shard_map/dot_general | solution.py:166
  235.3 338.2 %reduce-scatter.2.cloned.1.call-done = bf16[512,256]{1,0:T(8,128)(2,1)} async-done(((bf16[512,8192]{1,0:T(8,128)(2,1)}), bf16[512,256]{1,0:T(8,128)(2,1)}) %reduce-scatter.2.cloned.1.call-update) | async-done | bytes 262160 | tf_op jit(solution)/shard_map/reduce_scatter | solution.py:167
  (50 shorter events, 0.6 us)
Async XLA Ops:
  6.5 8.0 %copy-start.4 = (s32[1024,256]{1,0:T(8,128)S(1)}, s32[1024,256]{1,0:T(8,128)}, u32[]{:S(2)}) copy-start(s32[1024,256]{1,0:T(8,128)} %param.19) | copy-start | bytes 3145732
  6.5 7.9 %copy-start.6 = (bf16[64,256]{1,0:T(8,128)(2,1)S(1)}, bf16[64,256]{1,0:T(8,128)(2,1)}, u32[]{:S(2)}) copy-start(bf16[64,256]{1,0:T(8,128)(2,1)} %param.20) | copy-start | bytes 98308
  6.6 8.0 %copy-start.5 = (s32[1,1024,256]{2,1,0:T(8,128)S(1)}, s32[1,1024,256]{2,1,0:T(8,128)}, u32[]{:S(2)}) copy-start(s32[1,1024,256]{2,1,0:T(8,128)} %param.21) | copy-start | bytes 3145732
  6.6 7.9 %copy-start.7 = (bf16[1,64,256]{2,1,0:T(8,128)(2,1)S(1)}, bf16[1,64,256]{2,1,0:T(8,128)(2,1)}, u32[]{:S(2)}) copy-start(bf16[1,64,256]{2,1,0:T(8,128)(2,1)} %param.22) | copy-start | bytes 98308
  6.6 7.5 %copy-start.11 = (s32[16]{0:T(128)S(1)}, s32[16]{0:T(128)}, u32[]{:S(2)}) copy-start(s32[16]{0:T(128)} %param.26) | copy-start | bytes 196
  6.6 203.6 %all-gather.3.cloned.1.call-start = ((), (), s32[]{:S(2)}) async-start(), calls=%async_computation.2 | async-start | bytes 8650752 | tf_op jit(solution)/shard_map/all_gather | solution.py:139
  14.0 559.5 %reduce-scatter.2.cloned.1.call-start = ((), (), s32[]{:S(2)}) async-start(), calls=%async_computation.1 | async-start | bytes 8650752 | tf_op jit(solution)/shard_map/reduce_scatter | solution.py:167
  14.5 13.0 %copy-start.10 = (bf16[8192]{0:T(1024)(128)(2,1)S(1)}, bf16[8192]{0:T(1024)(128)(2,1)}, u32[]{:S(2)}) copy-start(bf16[8192]{0:T(1024)(128)(2,1)} %param.18) | copy-start | bytes 49156
  14.6 13.3 %copy-start = (s32[32]{0:T(128)S(1)}, s32[32]{0:T(128)}, u32[]{:S(2)}) copy-start(s32[32]{0:T(128)} %param.27) | copy-start | bytes 388
  21.0 8.9 %copy-start.8 = (bf16[2,8192]{1,0:T(2,128)(2,1)S(1)}, bf16[2,8192]{1,0:T(2,128)(2,1)}, u32[]{:S(2)}) copy-start(bf16[2,8192]{1,0:T(2,128)(2,1)} %param.24) | copy-start | bytes 98308
  21.0 9.0 %copy-start.9 = (s32[496,16]{0,1:T(8,128)S(1)}, s32[496,16]{0,1:T(8,128)}, u32[]{:S(2)}) copy-start(s32[496,16]{0,1:T(8,128)} %param.28) | copy-start | bytes 95236
  21.0 9.2 %copy-start.12 = (s32[496]{0:T(512)S(1)}, s32[496]{0:T(512)}, u32[]{:S(2)}) copy-start(s32[496]{0:T(512)} %param.29) | copy-start | bytes 5956
  21.0 9.9 %copy-start.3 = (s32[32,8192]{1,0:T(8,128)S(1)}, s32[32,8192]{1,0:T(8,128)}, u32[]{:S(2)}) copy-start(s32[32,8192]{1,0:T(8,128)} %param.23) | copy-start | bytes 3145732
  210.2 5.8 copy-start.1
  215.9 7.4 %copy-start.2 = (bf16[256,8192]{1,0:T(8,128)(2,1)S(1)}, bf16[256,8192]{1,0:T(8,128)(2,1)}, u32[]{:S(2)}) copy-start(bf16[256,8192]{1,0:T(8,128)(2,1)} %copy.64) | copy-start | bytes 12582916
  221.8 4.3 collective-permute-start
Sparse Core Ops, SparseCore 0:
  14.1 196.0 all-gather.2
  235.5 337.9 reduce-scatter.1
where the time goes:
time: 581 us; the launch traced here: 580 us
  waiting for transfers between devices  513 us (88%)
  local copies, waits for them, and re-layouts  17.8 us (3%)
  other arithmetic  17.3 us (3%)
  matrix products  16.7 us (3%)
  between operations  13.7 us (2%)
    reduce_scatter x1, waiting for transfers between devices, local(): lax.psum_scatter(partial_value.astype(jnp.bfloat16), 'tp', scatter_dimens...  338 us
    all_gather x1, waiting for transfers between devices, local(): whole = lax.all_gather(rows_in[0], 'tp', axis=1, tiled=True)  175 us
  transfers between devices with their start and end apart: 3, of which 2 were waited for; matrix products, arithmetic and copies ran while one was open for 4% of the time, Pallas kernels for 0%

commit v1 on v0

v1 whole, which is shorter than its diff:
```python
import functools

import jax
import jax.numpy as jnp
from jax import lax
from jax.experimental import pallas as pl
from jax.experimental.pallas import tpu as pltpu
from jax.sharding import PartitionSpec as P

HD = 128
LONGEST = 128
MESH = pl.DeviceIdType.MESH
VMEM = pltpu.VMEM


def nibble_order(width):
    words = width // 8
    source = lax.broadcasted_iota(jnp.int32, (width, width), 0)
    column = lax.broadcasted_iota(jnp.int32, (width, width), 1)
    wanted = lax.rem(column, words) * 8 + column // words
    return jnp.where(source == wanted, 1.0, 0.0).astype(jnp.bfloat16)


def unpack_into(target, lane, words, low_scale, high_scale):
    count, width = words.shape
    half = count // 2
    scale = jnp.concatenate(
        [
            jnp.broadcast_to(low_scale, (half, width)),
            jnp.broadcast_to(high_scale, (half, width)),
        ],
        axis=0,
    )
    for k in range(8):
        nibble = jnp.bitwise_and(jnp.right_shift(words, 4 * k), 15) - 8
        value = (nibble.astype(jnp.float32) * scale).astype(jnp.bfloat16)
        target[k * count : (k + 1) * count, lane : lane + width] = value


def ring(n):
    me = lax.axis_index("tp")
    return me, lax.rem(me + 1, n), lax.rem(me + n - 1, n)


def signal_ready(peers):
    barrier = pltpu.get_barrier_semaphore()
    for peer in peers:
        pl.semaphore_signal(barrier, inc=1, device_id=peer, device_id_type=MESH)
    return barrier


def gather_project(
    n, x_ref, q_words, kv_words, q_scales, kv_scales, gain_ref, cos_ref, sin_ref,
    q_out, kv_out, fresh_out,
    xbuf, stat, acc, weights, inverse, gains, scales, qw, kw, arrived,
    load_sem, recv_right, recv_left, stat_right, stat_left, send_sem, stat_send, pair_sem,
):
    me, right, left = ring(n)
    role = lax.axis_index("role")
    half, turn = n // 2, n // 4
    rows, width = x_ref.shape
    sub = rows // 4

    barrier = signal_ready(({"tp": right}, {"tp": left}, {"role": 1 - role}))
    loads = (
        pltpu.make_async_copy(q_words, qw, load_sem.at[0]),
        pltpu.make_async_copy(kv_words, kw, load_sem.at[1]),
    )
    for load in loads:
        load.start()

    order = nibble_order(width)
    x = x_ref[...]
    xbuf[me] = jnp.dot(x, order, preferred_element_type=jnp.float32).astype(jnp.bfloat16)
    wide = x.astype(jnp.float32)
    squares = wide * wide
    folded = squares[:, 0:128]
    for lane in range(128, width, 128):
        folded = folded + squares[:, lane : lane + 128]
    stat[me] = jnp.sum(folded.T, axis=0, keepdims=True)
    gains[...] = jnp.dot(gain_ref[...], order, preferred_element_type=jnp.float32)
    scales[:, 0:width] = q_scales[...].astype(jnp.float32)
    scales[:, width:] = kv_scales[...].astype(jnp.float32)
    acc[...] = jnp.zeros_like(acc)

    def data(chunk, hop, u, to_right):
        piece = xbuf.at[chunk, pl.ds(u * sub, sub), :]
        return pltpu.make_async_remote_copy(
            src_ref=piece,
            dst_ref=piece,
            send_sem=send_sem,
            recv_sem=(recv_right if to_right else recv_left).at[hop, u],
            device_id={"tp": right if to_right else left},
            device_id_type=MESH,
        )

    def figure(chunk, hop, to_right):
        return pltpu.make_async_remote_copy(
            src_ref=stat.at[chunk],
            dst_ref=stat.at[chunk],
            send_sem=stat_send,
            recv_sem=(stat_right if to_right else stat_left).at[hop],
            device_id={"tp": right if to_right else left},
            device_id_type=MESH,
        )

    def behind(s):
        return lax.rem(me + n - s, n)

    def ahead(s):
        return lax.rem(me + s, n)

    def pass_figures(h):
        figure(behind(h), h - 1, True).wait_recv()
        figure(behind(h), h, True).start()
        figure(ahead(h), h - 1, False).wait_recv()
        figure(ahead(h), h, False).start()

    def pass_data(s, u):
        data(behind(s), s - 1, u, True).wait_recv()
        data(behind(s), s, u, True).start()
        data(ahead(s), s - 1, u, False).wait_recv()
        data(ahead(s), s, u, False).start()

    def project(chunk):
        low = scales[pl.ds(2 * chunk, 1), :]
        high = scales[pl.ds(2 * chunk + 1, 1), :]
        first = pl.multiple_of(chunk * (width // 8), width // 8)
        for lane, words in ((0, qw), (width, kw)):
            unpack_into(
                weights, lane, words[pl.ds(first, width // 8), :],
                low[:, lane : lane + width], high[:, lane : lane + width],
            )
        gain = gains[pl.ds(chunk, 1), :]
        for u in range(4):
            part = pl.ds(u * sub, sub)
            scale = inverse[part, :]
            scale = jnp.concatenate([scale] * (width // 128), axis=1)
            normed = (xbuf[chunk, part, :].astype(jnp.float32) * scale * gain).astype(jnp.bfloat16)
            acc[part, :] += jnp.dot(normed, weights[...], preferred_element_type=jnp.float32)

    pl.semaphore_wait(barrier, 3)
    figure(me, 0, True).start()
    figure(me, 0, False).start()
    for u in range(4):
        data(me, 0, u, True).start()
        data(me, 0, u, False).start()
    for load in loads:
        load.wait()
    pass_figures(1)

    @pl.loop(1, turn)
    def _(s):
        for u in range(4):
            pass_data(s, u)
            if u == 1:
                pass_figures(2 * s)
            if u == 3:

                @pl.when(2 * s + 1 < half - 1)
                def _():
                    pass_figures(2 * s + 1)

                @pl.when(2 * s + 1 == half - 1)
                def _():
                    figure(behind(half - 1), half - 2, True).wait_recv()
                    figure(behind(half - 1), half - 1, True).start()
                    figure(ahead(half - 1), half - 2, False).wait_recv()

    figure(behind(half), half - 1, True).wait_recv()
    total = stat[0]
    for i in range(1, n):
        total = total + stat[i]
    mean = total / (n * width)
    inverse[...] = jnp.broadcast_to(lax.rsqrt(mean + 1e-05), (128, rows)).T

    @pl.loop(turn, half - 1)
    def _(s):
        for u in range(4):
            pass_data(s, u)
            o = 4 * (s - turn) + u
            project(behind((o + 1) // 2) if u % 2 else ahead(o // 2))

    last = half - 1
    for u in range(4):
        data(behind(last), last - 1, u, True).wait_recv()
        if u < 2:
            data(behind(last), last, u, True).start()
        data(ahead(last), last - 1, u, False).wait_recv()
        if u >= 2:
            data(ahead(last), last, u, False).start()
    project(ahead(last - 1))
    project(behind(last))
    project(ahead(last))
    for u in range(4):
        data(behind(half), last, u, u < 2).wait_recv()
    project(behind(half))

    cosine, sine = cos_ref[...], sin_ref[...]

    def rotated(lane):
        head = acc[:, lane : lane + HD]
        return (head * cosine + pltpu.roll(head, HD // 2, 1) * sine).astype(jnp.bfloat16)

    kv_out[:, 0:HD] = rotated(width)
    kv_out[:, HD:] = acc[:, width + HD :].astype(jnp.bfloat16)
    for lane in range(0, width, HD):
        q_out[:, lane : lane + HD] = rotated(lane)
    swap = pltpu.make_async_remote_copy(
        src_ref=kv_out, dst_ref=arrived, send_sem=pair_sem.at[0], recv_sem=pair_sem.at[1],
        device_id={"role": 1 - role}, device_id_type=MESH,
    )

    @pl.when(role == 0)
    def _():
        swap.start()
        fresh_out[...] = kv_out[...]
        swap.wait_send()

    @pl.when(role == 1)
    def _():
        swap.wait_recv()
        fresh_out[...] = arrived[...]

    every = xbuf.at[pl.ds(0, n - 1)]
    pltpu.make_async_copy(every, every, send_sem).wait()
    every = stat.at[pl.ds(0, n - 1)]
    pltpu.make_async_copy(every, every, stat_send).wait()


def project_scatter(
    n, att_ref, o_words, scale_ref, out_ref,
    attended, ow, weights, part, begun, slots, load_sem, recv_right, recv_left, send_sem,
):
    me, right, left = ring(n)
    half = n // 2
    rows, width = att_ref.shape
    sub = rows // 4
    barrier = signal_ready(({"tp": right}, {"tp": left}))
    load = pltpu.make_async_copy(o_words, ow, load_sem)
    load.start()
    attended[...] = jnp.dot(
        att_ref[...], nibble_order(width), preferred_element_type=jnp.float32
    ).astype(jnp.bfloat16)
    load.wait()

    def unpack(side, dest):
        columns = pl.ds(pl.multiple_of(dest * width, width), width)
        scale = scale_ref[:, columns].astype(jnp.float32)
        unpack_into(weights.at[side], 0, ow[:, columns], scale[0:1, :], scale[1:2, :])

    def multiply(side, u):
        piece = pl.ds(u * sub, sub)
        part[side, piece, :] = jnp.dot(
            attended[piece, :], weights[side], preferred_element_type=jnp.float32
        )

    def dest(side, s):
        return lax.rem(me + half + (s if side else n - s), n)

    def token(source, side, hop, u):
        piece = pl.ds(u * sub, sub)
        return pltpu.make_async_remote_copy(
            src_ref=source.at[piece, :],
            dst_ref=slots.at[side * half + hop, piece, :],
            send_sem=send_sem,
            recv_sem=(recv_left if side else recv_right).at[hop, u],
            device_id={"tp": left if side else right},
            device_id_type=MESH,
        )

    def slot(side, hop):
        return slots.at[side * half + hop]

    unpack(0, dest(0, 0))
    for u in range(4):
        multiply(0, u)
    begun[...] = part[0].astype(jnp.bfloat16)
    pl.semaphore_wait(barrier, 2)
    for u in range(4):
        token(begun, u // 2, 0, u).start()
    for side in range(2):
        unpack(side, dest(side, 1))
        for u in range(4):
            multiply(side, u)

    def step(s, joins):
        for side in range(2):
            unpack(side, dest(side, s + 1))
        for u in range(4):
            piece = pl.ds(u * sub, sub)
            for side in range(2):
                here = slot(side, s - 1)
                term = part[side, piece, :]
                if joins(side, u):
                    token(here, side, s - 1, u).wait_recv()
                    term = term + here[piece, :].astype(jnp.float32)
                here[piece, :] = term.astype(jnp.bfloat16)
                multiply(side, u)
                token(here, side, s, u).start()

    step(1, lambda side, u: side == u // 2)

    @pl.loop(2, half)
    def _(s):
        step(s, lambda side, u: True)

    for u in range(4):
        piece = pl.ds(u * sub, sub)
        term = part[0, piece, :]
        for side in range(2):
            here = slot(side, half - 1)
            token(here, side, half - 1, u).wait_recv()
            term = term + here[piece, :].astype(jnp.float32)
        out_ref[piece, :] = term.astype(jnp.bfloat16)
    every = slots.at[pl.ds(0, n - 1)]
    pltpu.make_async_copy(every, every, send_sem).wait()


def prefill_kernel(start_ref, q_ref, kv_ref, out_ref):
    rows = q_ref.shape[0]
    block = min(LONGEST, rows)
    for first in range(0, rows, block):
        low = max(0, first - LONGEST)
        count = first + block - low
        keys = kv_ref[low : first + block, 0:HD]
        values = kv_ref[low : first + block, HD:]
        row = lax.broadcasted_iota(jnp.int32, (block, count), 0) + first
        key = lax.broadcasted_iota(jnp.int32, (block, count), 1) + low
        allowed = (key <= row) & (key >= start_ref[first : first + block, :])
        for lane in range(0, q_ref.shape[1], HD):
            query = q_ref[first : first + block, lane : lane + HD]
            scores = lax.dot_general(
                query, keys, (((1,), (1,)), ((), ())), preferred_element_type=jnp.float32
            ) * (HD**-0.5)
            scores = jnp.where(allowed, scores, -1e30)
            top = jnp.max(scores, axis=1, keepdims=True)
            raised = jnp.exp(scores - top)
            weight = raised * (1.0 / jnp.sum(raised, axis=1, keepdims=True))
            out_ref[first : first + block, lane : lane + HD] = jnp.dot(
                weight.astype(jnp.bfloat16), values, preferred_element_type=jnp.float32
            ).astype(jnp.bfloat16)


def decode_kernel(
    table_ref, length_ref, q_ref, kv_ref, fresh_ref, pool_ref, out_ref,
    cache, q_wide, kv_wide, out_wide, load_sem,
):
    rows = q_ref.shape[0]
    pool, page, _ = pool_ref.shape
    span = table_ref.shape[0] // rows
    load = pltpu.make_async_copy(pool_ref, cache.at[pl.ds(0, pool)], load_sem)
    load.start()
    for j in range(rows // page):
        cache[pool + j] = fresh_ref[j * page : (j + 1) * page, :]
    q_wide[...] = q_ref[...].astype(jnp.float32)
    kv_wide[...] = kv_ref[...].astype(jnp.float32)
    load.wait()
    batch = 8
    owner = lax.rem(lax.broadcasted_iota(jnp.int32, (2 * batch, HD), 0), batch)
    spot = lax.broadcasted_iota(jnp.int32, (2 * batch, span * page), 1)

    def gathered(first, lane):
        pages = []
        for j in range(span):
            pair = [
                cache[table_ref[(first + t) * span + j], :, lane : lane + HD] for t in range(2)
            ]
            pages.append(jnp.concatenate(pair, axis=1))
        return jnp.concatenate(pages, axis=0)

    def one_block(b):
        first = pl.multiple_of(b * batch, batch)
        piece = pl.ds(first, batch)
        both = q_wide[piece, :]
        query = jnp.concatenate([both[:, 0:HD], both[:, HD:]], axis=0)
        own = kv_wide[piece, :]
        own_key = jnp.concatenate([own[:, 0:HD]] * 2, axis=0)
        own_value = jnp.concatenate([own[:, HD:]] * 2, axis=0)
        length = length_ref[piece, :]
        length = jnp.concatenate([length] * 2, axis=0)
        scores = None
        for p in range(0, batch, 2):
            mine = jnp.concatenate(
                [jnp.where(owner == p + t, query, 0.0) for t in range(2)], axis=1
            ).astype(jnp.bfloat16)
            term = lax.dot_general(
                mine, gathered(first + p, 0), (((1,), (1,)), ((), ())),
                preferred_element_type=jnp.float32,
            )
            scores = term if scores is None else scores + term
        scores = jnp.where(spot < length, scores * (HD**-0.5), -1e30)
        self_score = jnp.sum(query * own_key, axis=1, keepdims=True) * (HD**-0.5)
        top = jnp.maximum(jnp.max(scores, axis=1, keepdims=True), self_score)
        raised = jnp.exp(scores - top)
        self_raised = jnp.exp(self_score - top)
        share = 1.0 / (jnp.sum(raised, axis=1, keepdims=True) + self_raised)
        weight = (raised * share).astype(jnp.bfloat16)
        total = (self_raised * share).astype(jnp.bfloat16).astype(jnp.float32) * own_value
        for p in range(0, batch, 2):
            term = jnp.dot(weight, gathered(first + p, HD), preferred_element_type=jnp.float32)
            for t in range(2):
                total = total + jnp.where(owner == p + t, term[:, t * HD : (t + 1) * HD], 0.0)
        out_wide[piece, 0:HD] = total[0:batch, :]
        out_wide[piece, HD:] = total[batch:, :]

    @pl.loop(0, rows // batch, step=2)
    def _(b):
        one_block(b)
        one_block(b + 1)

    out_ref[...] = out_wide[...].astype(jnp.bfloat16)


def local(
    rows_in, norm_gain, q_words, q_scales, kv_words, kv_scales, o_words, o_scales,
    kv_pool, prompt_pages, page_slots, block_tables, cache_lens,
):
    n = lax.axis_size("tp")
    side = lax.axis_index("role")
    x = rows_in[0]
    rows, width = x.shape
    half = n // 2
    pool = kv_pool[0]
    page = pool.shape[1]
    count = prompt_pages.shape[0]
    sub_sems = pltpu.SemaphoreType.DMA((half, 4))
    dma = pltpu.SemaphoreType.DMA
    in_vmem = pl.BlockSpec(memory_space=VMEM)
    anywhere = pl.BlockSpec(memory_space=pl.ANY)
    bf16, f32 = jnp.bfloat16, jnp.float32

    ends = jnp.cumsum(prompt_pages) * page
    starts = ends - prompt_pages * page
    index = jnp.arange(rows, dtype=jnp.int32)
    member = (index[:, None] >= starts[None, :]) & (index[:, None] < ends[None, :])
    doc_start = jnp.sum(jnp.where(member, starts[None, :], 0), axis=1)
    lengths = jnp.concatenate([prompt_pages * page, cache_lens])
    positions = jnp.where(side == 0, index - doc_start, lengths)
    freq = 500000.0 ** (-jnp.arange(HD // 2, dtype=f32) * 2.0 / HD)
    angle = positions.astype(f32)[:, None] * freq[None, :]
    cosine, sine = jnp.cos(angle), jnp.sin(angle)
    cosine = jnp.concatenate([cosine, cosine], axis=1)
    sine = jnp.concatenate([-sine, sine], axis=1)

    half_block = jax.ShapeDtypeStruct((rows, width), bf16)
    query, fresh, arrived = pl.pallas_call(
        functools.partial(gather_project, n),
        out_shape=(half_block, jax.ShapeDtypeStruct((rows, 2 * HD), bf16),
                   jax.ShapeDtypeStruct((rows, 2 * HD), bf16)),
        in_specs=[in_vmem, anywhere, anywhere] + [in_vmem] * 5,
        out_specs=(in_vmem, in_vmem, in_vmem),
        scratch_shapes=[
            VMEM((n, rows, width), bf16),
            VMEM((n, 1, rows), f32),
            VMEM((rows, width + 2 * HD), f32),
            VMEM((width, width + 2 * HD), bf16),
            VMEM((rows, 128), f32),
            VMEM((n, width), f32),
            VMEM((q_scales.shape[0], width + 2 * HD), f32),
            VMEM(q_words.shape, jnp.int32),
            VMEM(kv_words.shape[1:], jnp.int32),
            VMEM((rows, 2 * HD), bf16),
            dma((2,)), sub_sems, sub_sems, dma((half,)), dma((half,)),
            dma, dma, dma((2,)),
        ],
        compiler_params=pltpu.CompilerParams(
            collective_id=0, has_side_effects=True, vmem_limit_bytes=40 << 20
        ),
        cost_estimate=pl.CostEstimate(
            flops=4 * n * rows * width * width, bytes_accessed=4 << 20, transcendentals=0
        ),
        name="gather_project",
    )(
        x, q_words, kv_words[0], q_scales, kv_scales[0],
        norm_gain.reshape(n, width), cosine, sine,
    )

    def run_prefill():
        return pl.pallas_call(
            prefill_kernel,
            out_shape=half_block,
            in_specs=[in_vmem] * 3,
            out_specs=in_vmem,
            name="prefill",
        )(doc_start[:, None], query, fresh)

    def run_decode():
        span = block_tables.shape[1]
        own = pool.shape[0] + jnp.minimum(
            starts[:, None] // page + jnp.arange(span, dtype=jnp.int32)[None, :],
            page_slots.shape[0] - 1,
        )
        table = jnp.concatenate([own, block_tables], axis=0).reshape(-1)
        return pl.pallas_call(
            decode_kernel,
            out_shape=half_block,
            in_specs=[pl.BlockSpec(memory_space=pltpu.SMEM)] + [in_vmem] * 4 + [anywhere],
            out_specs=in_vmem,
            scratch_shapes=[
                VMEM((pool.shape[0] + rows // page, page, 2 * HD), bf16),
                VMEM((rows, width), f32),
                VMEM((rows, 2 * HD), f32),
                VMEM((rows, width), f32),
                dma,
            ],
            compiler_params=pltpu.CompilerParams(vmem_limit_bytes=40 << 20),
            name="decode",
        )(table, lengths[:, None], query, fresh, arrived, pool)

    attended = lax.cond(side == 0, run_prefill, run_decode)

    out = pl.pallas_call(
        functools.partial(project_scatter, n),
        out_shape=half_block,
        in_specs=[in_vmem, anywhere, in_vmem],
        out_specs=in_vmem,
        scratch_shapes=[
            VMEM((rows, width), bf16),
            VMEM(o_words.shape, jnp.int32),
            VMEM((2, width, width), bf16),
            VMEM((2, rows, width), f32),
            VMEM((rows, width), bf16),
            VMEM((n, rows, width), bf16),
            dma, sub_sems, sub_sems, dma,
        ],
        compiler_params=pltpu.CompilerParams(
            collective_id=1, has_side_effects=True, vmem_limit_bytes=40 << 20
        ),
        cost_estimate=pl.CostEstimate(
            flops=2 * n * rows * width * width, bytes_accessed=4 << 20, transcendentals=0
        ),
        name="project_scatter",
    )(attended, o_words, o_scales)
    return out[None]


def solution(mesh):
    return jax.shard_map(
        local,
        mesh=mesh,
        in_specs=(
            P("role", "groups", "tp"),
            P(),
            P(None, "tp"),
            P(None, "tp"),
            P("tp", None, None),
            P("tp", None, None),
            P("tp", None),
            P("tp", None),
            P("tp", "groups", None, None),
            P("groups"),
            P("groups"),
            P("groups", None),
            P("groups"),
        ),
        out_specs=P("role", "groups", "tp"),
        check_vma=False,
    )
```

time: 581 us -> 243 us (0.42)
  the two profiles are of different devices: /device:TPU:38 before, /device:TPU:37 now
where the time goes in v1:
time: 243 us
  Pallas kernels  232 us (95%)
  local copies, waits for them, and re-layouts  7.5 us (3%)
  other arithmetic  2.96 us (1%)
    pallas_call x1, Pallas kernels, local(): pl.pallas_call(functools.partial(gather_project, n), out_shape=(half_bloc...  121 us
    pallas_call x1, Pallas kernels, local(): pl.pallas_call(functools.partial(project_scatter, n), out_shape=half_bloc...  60.8 us
    pallas_call x1, Pallas kernels, run_decode(): pl.pallas_call(decode_kernel, out_shape=half_block, in_specs=[pl.BlockSpe...  50.7 us
    unnamed x17, local copies, waits for them, and re-layouts  5.63 us

profile of v1, /device:TPU:37, one launch (start us, length us, event | category | flops | bytes accessed | tf_op | source)
XLA Modules:
  0.0 242.8 jit_solution(4435287103602441445)
XLA Ops:
  0.0 0.7 copy.27
  0.8 0.1 multiply_reduce_fusion
  0.9 0.7 broadcast_multiply_fusion
  1.6 0.1 select_reduce_fusion
  1.7 0.8 select_convert_fusion
  2.4 0.7 reshape.76.gain_ref
  3.1 1.0 fusion
  4.1 0.0 copy-start.7
  4.2 0.2 pad_maximum_fusion
  4.4 0.0 copy-start
  4.4 1.2 copy-done
  5.6 0.0 copy-start.1
  5.6 1.2 copy-done.1
  6.8 0.0 copy-start.3
  6.8 0.9 copy-done.3
  7.8 0.0 copy-start.4
  7.8 0.8 copy-done.4
  8.5 0.8 copy-done.5
  9.3 120.7 %gather_project.1 = (bf16[512,256]{1,0:T(8,128)(2,1)S(1)}, bf16[512,256]{1,0:T(8,128)(2,1)S(1)}, bf16[512,256]{1,0:T(8,128)(2,1)S(1)}) custom-call(bf16[512,256]{1,0:T(8,128)(2,1)S(1)} %bitcast.10, s32[1024,256]{1,0:T(8,128)S(1)} %copy-done, s32[1024,256]{1,0:T(8,128)S(1)} %bitcast.9, bf16[64,256]{1,0:T(8,128)(2,1)S(1)} %copy-done.4, ...), custom_call_target="tpu_custom_call" | custom-call | flops 4294967296 | bytes 4194304 | tf_op jit(solution)/shard_map/gather_project/pallas_call | solution.py:447
  130.0 0.0 copy-start.2
  130.0 0.0 copy-start.6
  130.0 0.0 copy-done.7
  130.0 51.3 %conditional.1 = (bf16[512,256]{1,0:T(8,128)(2,1)S(1)}) conditional(s32[]{:T(128)} %convert_element_type.10, (s32[16]{0:T(128)S(1)}, s32[496,16]{0,1:T(8,128)S(1)}, s32[512]{0:T(512)S(1)}, bf16[1,1024,16,256]{3,2,1,0:T(8,128)(2,1)}, bf16[512,256]{1,0:T(8,128)(2,1)S(1)}, /*index=5*/bf16[512,256]{1,0:T(8,128)(2,1)S(1)}, ...), branch_computations={%region_2.3_spmd, %region_3.4_spmd} | conditional | flops 9200 | bytes 201928 | solution.py:511
  130.1 0.1 pad_add_fusion
  130.1 0.1 copy.24
  130.3 0.1 reshape.72.table_ref
  130.4 0.1 copy.25.length_ref
  130.6 50.7 %decode.1 = bf16[512,256]{1,0:T(8,128)(2,1)S(1)} custom-call(s32[8192]{0:T(1024)S(1)} %reshape.72.table_ref, s32[512,1]{1,0:T(8,128)S(1)} %copy.25.length_ref, bf16[512,256]{1,0:T(8,128)(2,1)S(1)} %get-tuple-element.32.q_ref, bf16[512,256]{1,0:T(8,128)(2,1)S(1)} %get-tuple-element.33.kv_ref, bf16[512,256]{1,0:T(8,128)(2,1)S(1)} %get-tuple-element.34.fresh_ref, ...), custom_call_target="tpu_custom_call" | custom-call | tf_op jit(solution)/shard_map/cond/branch_0_fun/decode/pallas_call | solution.py:495
  181.3 0.0 copy-done.2
  181.3 0.0 copy-done.6
  181.3 60.8 %project_scatter.1 = bf16[512,256]{1,0:T(8,128)(2,1)S(1)} custom-call(bf16[512,256]{1,0:T(8,128)(2,1)S(1)} %get-tuple-element.65.att_ref, s32[32,8192]{1,0:T(8,128)S(1)} %copy-done.2, bf16[2,8192]{1,0:T(2,128)(2,1)S(1)} %copy-done.6), custom_call_target="tpu_custom_call" | custom-call | flops 2147483648 | bytes 4194304 | tf_op jit(solution)/shard_map/project_scatter/pallas_call | solution.py:513
  242.1 0.7 copy.31
  (5 shorter events, 0.1 us)
Async XLA Ops:
  4.1 125.9 %copy-start.7 = (s32[496,16]{0,1:T(8,128)S(1)}, s32[496,16]{0,1:T(8,128)}, u32[]{:S(2)}) copy-start(s32[496,16]{0,1:T(8,128)} %param.25) | copy-start | bytes 95236
  4.4 1.2 copy-start
  5.6 1.2 copy-start.1
  6.8 0.9 copy-start.3
  7.8 0.8 copy-start.4
  8.5 0.8 copy-start.5
  130.0 51.3 %copy-start.2 = (s32[32,8192]{1,0:T(8,128)S(1)}, s32[32,8192]{1,0:T(8,128)}, u32[]{:S(2)}) copy-start(s32[32,8192]{1,0:T(8,128)} %o_words.1) | copy-start | bytes 3145732
  130.0 51.3 %copy-start.6 = (bf16[2,8192]{1,0:T(2,128)(2,1)S(1)}, bf16[2,8192]{1,0:T(2,128)(2,1)}, u32[]{:S(2)}) copy-start(bf16[2,8192]{1,0:T(2,128)(2,1)} %scale_ref.1) | copy-start | bytes 98308

commit v2 on v1

--- a/solution.py
+++ b/solution.py
@@ -2,6 +2,7 @@
 
 import jax
 import jax.numpy as jnp
+import numpy as np
 from jax import lax
 from jax.experimental import pallas as pl
 from jax.experimental.pallas import tpu as pltpu
@@ -9,6 +10,9 @@
 
 HD = 128
 LONGEST = 128
+GATHER_PIECES = 4
+SCATTER_PIECES = 8
+GATHER_VMEM = 58 << 20
 MESH = pl.DeviceIdType.MESH
 VMEM = pltpu.VMEM
 
@@ -49,27 +53,40 @@
     return barrier
 
 
+def prompt_start(pages_ref, page, row):
+    start, begin = jnp.zeros_like(row), 0
+    for p in range(pages_ref.shape[0]):
+        end = begin + pages_ref[p] * page
+        start = jnp.where((row >= begin) & (row < end), begin, start)
+        begin = end
+    return start
+
+
 def gather_project(
-    n, x_ref, q_words, kv_words, q_scales, kv_scales, gain_ref, cos_ref, sin_ref,
-    q_out, kv_out, fresh_out,
-    xbuf, stat, acc, weights, inverse, gains, scales, qw, kw, arrived,
+    page, n, pages_ref, x_hbm, q_words, kv_words, q_scales, kv_scales, gain_ref,
+    length_ref, freq_ref, q_out, kv_out, fresh_out,
+    x_ref, xbuf, stat, acc, weights, inverse, gains, scales, qw, kw, arrived, cosine, sine,
     load_sem, recv_right, recv_left, stat_right, stat_left, send_sem, stat_send, pair_sem,
 ):
     me, right, left = ring(n)
     role = lax.axis_index("role")
     half, turn = n // 2, n // 4
     rows, width = x_ref.shape
-    sub = rows // 4
+    pieces = recv_right.shape[1]
+    sub = rows // pieces
 
     barrier = signal_ready(({"tp": right}, {"tp": left}, {"role": 1 - role}))
+    load_x = pltpu.make_async_copy(x_hbm, x_ref, load_sem.at[0])
     loads = (
-        pltpu.make_async_copy(q_words, qw, load_sem.at[0]),
-        pltpu.make_async_copy(kv_words, kw, load_sem.at[1]),
+        pltpu.make_async_copy(q_words, qw, load_sem.at[1]),
+        pltpu.make_async_copy(kv_words, kw, load_sem.at[2]),
     )
+    load_x.start()
     for load in loads:
         load.start()
 
     order = nibble_order(width)
+    load_x.wait()
     x = x_ref[...]
     xbuf[me] = jnp.dot(x, order, preferred_element_type=jnp.float32).astype(jnp.bfloat16)
     wide = x.astype(jnp.float32)
@@ -78,10 +95,6 @@
     for lane in range(128, width, 128):
         folded = folded + squares[:, lane : lane + 128]
     stat[me] = jnp.sum(folded.T, axis=0, keepdims=True)
-    gains[...] = jnp.dot(gain_ref[...], order, preferred_element_type=jnp.float32)
-    scales[:, 0:width] = q_scales[...].astype(jnp.float32)
-    scales[:, width:] = kv_scales[...].astype(jnp.float32)
-    acc[...] = jnp.zeros_like(acc)
 
     def data(chunk, hop, u, to_right):
         piece = xbuf.at[chunk, pl.ds(u * sub, sub), :]
@@ -133,7 +146,7 @@
             )
         gain = gains[pl.ds(chunk, 1), :]
         for u in range(4):
-            part = pl.ds(u * sub, sub)
+            part = pl.ds(u * (rows // 4), rows // 4)
             scale = inverse[part, :]
             scale = jnp.concatenate([scale] * (width // 128), axis=1)
             normed = (xbuf[chunk, part, :].astype(jnp.float32) * scale * gain).astype(jnp.bfloat16)
@@ -142,20 +155,36 @@
     pl.semaphore_wait(barrier, 3)
     figure(me, 0, True).start()
     figure(me, 0, False).start()
-    for u in range(4):
+    for u in range(pieces):
         data(me, 0, u, True).start()
         data(me, 0, u, False).start()
+    gains[...] = jnp.dot(
+        gain_ref[...].astype(jnp.bfloat16), order, preferred_element_type=jnp.float32
+    )
+    scales[:, 0:width] = q_scales[...].astype(jnp.float32)
+    scales[:, width:] = kv_scales[...].astype(jnp.float32)
+    acc[...] = jnp.zeros_like(acc)
+    row = lax.broadcasted_iota(jnp.int32, (rows, HD), 0)
+    placed = (row - prompt_start(pages_ref, page, row)).astype(jnp.float32)
+    held = jnp.broadcast_to(length_ref[...].astype(jnp.float32), (HD, rows)).T
+    angle = jnp.where(role == 0, placed, held) * freq_ref[...]
+    cosine[...] = jnp.cos(angle)
+    turned = jnp.sin(angle)
+    lane = lax.broadcasted_iota(jnp.int32, (rows, HD), 1)
+    sine[...] = jnp.where(lane < HD // 2, -turned, turned)
     for load in loads:
         load.wait()
     pass_figures(1)
 
+    quarter = pieces // 4
+
     @pl.loop(1, turn)
     def _(s):
-        for u in range(4):
+        for u in range(pieces):
             pass_data(s, u)
-            if u == 1:
+            if u == 2 * quarter - 1:
                 pass_figures(2 * s)
-            if u == 3:
+            if u == pieces - 1:
 
                 @pl.when(2 * s + 1 < half - 1)
                 def _():
@@ -176,31 +205,31 @@
 
     @pl.loop(turn, half - 1)
     def _(s):
-        for u in range(4):
-            pass_data(s, u)
-            o = 4 * (s - turn) + u
-            project(behind((o + 1) // 2) if u % 2 else ahead(o // 2))
+        for i in range(4):
+            for u in range(i * quarter, (i + 1) * quarter):
+                pass_data(s, u)
+            o = 4 * (s - turn) + i
+            project(behind((o + 1) // 2) if i % 2 else ahead(o // 2))
 
     last = half - 1
-    for u in range(4):
+    for u in range(pieces):
         data(behind(last), last - 1, u, True).wait_recv()
-        if u < 2:
+        if u < pieces // 2:
             data(behind(last), last, u, True).start()
         data(ahead(last), last - 1, u, False).wait_recv()
-        if u >= 2:
+        if u >= pieces // 2:
             data(ahead(last), last, u, False).start()
     project(ahead(last - 1))
     project(behind(last))
     project(ahead(last))
-    for u in range(4):
-        data(behind(half), last, u, u < 2).wait_recv()
+    for u in range(pieces):
+        data(behind(half), last, u, u < pieces // 2).wait_recv()
     project(behind(half))
-
-    cosine, sine = cos_ref[...], sin_ref[...]
 
     def rotated(lane):
         head = acc[:, lane : lane + HD]
-        return (head * cosine + pltpu.roll(head, HD // 2, 1) * sine).astype(jnp.bfloat16)
+        turned = pltpu.roll(head, HD // 2, 1)
+        return (head * cosine[...] + turned * sine[...]).astype(jnp.bfloat16)
 
     kv_out[:, 0:HD] = rotated(width)
     kv_out[:, HD:] = acc[:, width + HD :].astype(jnp.bfloat16)
@@ -235,7 +264,8 @@
     me, right, left = ring(n)
     half = n // 2
     rows, width = att_ref.shape
-    sub = rows // 4
+    pieces = recv_right.shape[1]
+    sub = rows // pieces
     barrier = signal_ready(({"tp": right}, {"tp": left}))
     load = pltpu.make_async_copy(o_words, ow, load_sem)
     load.start()
@@ -249,10 +279,10 @@
         scale = scale_ref[:, columns].astype(jnp.float32)
         unpack_into(weights.at[side], 0, ow[:, columns], scale[0:1, :], scale[1:2, :])
 
-    def multiply(side, u):
-        piece = pl.ds(u * sub, sub)
-        part[side, piece, :] = jnp.dot(
-            attended[piece, :], weights[side], preferred_element_type=jnp.float32
+    def multiply(side, turn, i):
+        block = pl.ds(i * (rows // 2), rows // 2)
+        part[turn, side, block, :] = jnp.dot(
+            attended[block, :], weights[side], preferred_element_type=jnp.float32
         )
 
     def dest(side, s):
@@ -273,41 +303,48 @@
         return slots.at[side * half + hop]
 
     unpack(0, dest(0, 0))
-    for u in range(4):
-        multiply(0, u)
-    begun[...] = part[0].astype(jnp.bfloat16)
+    for i in range(2):
+        multiply(0, 0, i)
+    begun[...] = part[0, 0].astype(jnp.bfloat16)
     pl.semaphore_wait(barrier, 2)
-    for u in range(4):
-        token(begun, u // 2, 0, u).start()
+    for u in range(pieces):
+        token(begun, 2 * u // pieces, 0, u).start()
     for side in range(2):
         unpack(side, dest(side, 1))
-        for u in range(4):
-            multiply(side, u)
+        for i in range(2):
+            multiply(side, 1, i)
+
+    def ahead(s, turn, task):
+        side = task % 2
+        if task < 2:
+            unpack(side, dest(side, s))
+        else:
+            multiply(side, turn, (task - 2) // 2)
 
     def step(s, joins):
-        for side in range(2):
-            unpack(side, dest(side, s + 1))
-        for u in range(4):
+        now, later = lax.rem(s, 2), lax.rem(s + 1, 2)
+        for u in range(pieces):
             piece = pl.ds(u * sub, sub)
             for side in range(2):
                 here = slot(side, s - 1)
-                term = part[side, piece, :]
+                term = part[now, side, piece, :]
                 if joins(side, u):
                     token(here, side, s - 1, u).wait_recv()
                     term = term + here[piece, :].astype(jnp.float32)
                 here[piece, :] = term.astype(jnp.bfloat16)
-                multiply(side, u)
                 token(here, side, s, u).start()
-
-    step(1, lambda side, u: side == u // 2)
+            for task in range(6 * u // pieces, 6 * (u + 1) // pieces):
+                ahead(s + 1, later, task)
+
+    step(1, lambda side, u: side == 2 * u // pieces)
 
     @pl.loop(2, half)
     def _(s):
         step(s, lambda side, u: True)
 
-    for u in range(4):
+    for u in range(pieces):
         piece = pl.ds(u * sub, sub)
-        term = part[0, piece, :]
+        term = part[half % 2, 0, piece, :]
         for side in range(2):
             here = slot(side, half - 1)
             token(here, side, half - 1, u).wait_recv()
@@ -317,7 +354,7 @@
     pltpu.make_async_copy(every, every, send_sem).wait()
 
 
-def prefill_kernel(start_ref, q_ref, kv_ref, out_ref):
+def prefill_kernel(page, pages_ref, q_ref, kv_ref, out_ref):
     rows = q_ref.shape[0]
     block = min(LONGEST, rows)
     for first in range(0, rows, block):
@@ -327,7 +364,8 @@
         values = kv_ref[low : first + block, HD:]
         row = lax.broadcasted_iota(jnp.int32, (block, count), 0) + first
         key = lax.broadcasted_iota(jnp.int32, (block, count), 1) + low
-        allowed = (key <= row) & (key >= start_ref[first : first + block, :])
+        start = prompt_start(pages_ref, page, row)
+        allowed = (key <= row) & (key >= start)
         for lane in range(0, q_ref.shape[1], HD):
             query = q_ref[first : first + block, lane : lane + HD]
             scores = lax.dot_general(
@@ -342,9 +380,22 @@
             ).astype(jnp.bfloat16)
 
 
+def decode_scratch(rows, width, tokens, pages, page):
+    return [
+        VMEM((pages, page, 2 * HD), jnp.bfloat16),
+        VMEM((rows, width), jnp.float32),
+        VMEM((rows, 2 * HD), jnp.float32),
+        VMEM((2 * rows, tokens), jnp.float32),
+        VMEM((2 * rows, HD), jnp.float32),
+        VMEM((2 * rows, tokens), jnp.bfloat16),
+        VMEM((rows, width), jnp.float32),
+        pltpu.SemaphoreType.DMA,
+    ]
+
+
 def decode_kernel(
     table_ref, length_ref, q_ref, kv_ref, fresh_ref, pool_ref, out_ref,
-    cache, q_wide, kv_wide, out_wide, load_sem,
+    cache, q_wide, kv_wide, score_buf, self_buf, weight_buf, out_wide, load_sem,
 ):
     rows = q_ref.shape[0]
     pool, page, _ = pool_ref.shape
@@ -369,16 +420,15 @@
             pages.append(jnp.concatenate(pair, axis=1))
         return jnp.concatenate(pages, axis=0)
 
-    def one_block(b):
+    def twice(piece, ref, lane):
+        return jnp.concatenate([ref[piece, lane : lane + HD]] * 2, axis=0)
+
+    def score_block(b):
         first = pl.multiple_of(b * batch, batch)
         piece = pl.ds(first, batch)
         both = q_wide[piece, :]
         query = jnp.concatenate([both[:, 0:HD], both[:, HD:]], axis=0)
-        own = kv_wide[piece, :]
-        own_key = jnp.concatenate([own[:, 0:HD]] * 2, axis=0)
-        own_value = jnp.concatenate([own[:, HD:]] * 2, axis=0)
-        length = length_ref[piece, :]
-        length = jnp.concatenate([length] * 2, axis=0)
+        length = jnp.concatenate([length_ref[piece, :]] * 2, axis=0)
         scores = None
         for p in range(0, batch, 2):
             mine = jnp.concatenate(
@@ -389,14 +439,29 @@
                 preferred_element_type=jnp.float32,
             )
             scores = term if scores is None else scores + term
-        scores = jnp.where(spot < length, scores * (HD**-0.5), -1e30)
-        self_score = jnp.sum(query * own_key, axis=1, keepdims=True) * (HD**-0.5)
+        out = pl.ds(2 * first, 2 * batch)
+        score_buf[out, :] = jnp.where(spot < length, scores * (HD**-0.5), -1e30)
+        self_score = jnp.sum(query * twice(piece, kv_wide, 0), axis=1, keepdims=True)
+        self_buf[out, :] = jnp.broadcast_to(self_score * (HD**-0.5), (2 * batch, HD))
+
+    def weigh(i):
+        piece = pl.ds(i * 128, 128)
+        scores, self_score = score_buf[piece, :], self_buf[piece, :]
         top = jnp.maximum(jnp.max(scores, axis=1, keepdims=True), self_score)
-        raised = jnp.exp(scores - top)
+        raised = jnp.exp(scores - jnp.concatenate([top] * (scores.shape[1] // HD), axis=1))
         self_raised = jnp.exp(self_score - top)
         share = 1.0 / (jnp.sum(raised, axis=1, keepdims=True) + self_raised)
-        weight = (raised * share).astype(jnp.bfloat16)
-        total = (self_raised * share).astype(jnp.bfloat16).astype(jnp.float32) * own_value
+        share = jnp.broadcast_to(share, self_score.shape)
+        weight_buf[piece, :] = (
+            raised * jnp.concatenate([share] * (scores.shape[1] // HD), axis=1)
+        ).astype(jnp.bfloat16)
+        self_buf[piece, :] = (self_raised * share).astype(jnp.bfloat16).astype(jnp.float32)
+
+    def value_block(b):
+        first = pl.multiple_of(b * batch, batch)
+        piece = pl.ds(first, batch)
+        weight = weight_buf[pl.ds(2 * first, 2 * batch), :]
+        total = self_buf[pl.ds(2 * first, 2 * batch), :] * twice(piece, kv_wide, HD)
         for p in range(0, batch, 2):
             term = jnp.dot(weight, gathered(first + p, HD), preferred_element_type=jnp.float32)
             for t in range(2):
@@ -404,10 +469,19 @@
         out_wide[piece, 0:HD] = total[0:batch, :]
         out_wide[piece, HD:] = total[batch:, :]
 
-    @pl.loop(0, rows // batch, step=2)
+    @pl.loop(0, rows // batch, step=4)
     def _(b):
-        one_block(b)
-        one_block(b + 1)
+        for i in range(4):
+            score_block(b + i)
+
+    @pl.loop(0, 2 * rows // 128)
+    def _(i):
+        weigh(i)
+
+    @pl.loop(0, rows // batch, step=4)
+    def _(b):
+        for i in range(4):
+            value_block(b + i)
 
     out_ref[...] = out_wide[...].astype(jnp.bfloat16)
 
@@ -424,33 +498,29 @@
     pool = kv_pool[0]
     page = pool.shape[1]
     count = prompt_pages.shape[0]
-    sub_sems = pltpu.SemaphoreType.DMA((half, 4))
     dma = pltpu.SemaphoreType.DMA
+    gather_sems, scatter_sems = dma((half, GATHER_PIECES)), dma((half, SCATTER_PIECES))
     in_vmem = pl.BlockSpec(memory_space=VMEM)
-    anywhere = pl.BlockSpec(memory_space=pl.ANY)
+    in_smem = pl.BlockSpec(memory_space=pltpu.SMEM)
+    in_hbm = pl.BlockSpec(memory_space=pltpu.HBM)
     bf16, f32 = jnp.bfloat16, jnp.float32
 
-    ends = jnp.cumsum(prompt_pages) * page
-    starts = ends - prompt_pages * page
-    index = jnp.arange(rows, dtype=jnp.int32)
-    member = (index[:, None] >= starts[None, :]) & (index[:, None] < ends[None, :])
-    doc_start = jnp.sum(jnp.where(member, starts[None, :], 0), axis=1)
     lengths = jnp.concatenate([prompt_pages * page, cache_lens])
-    positions = jnp.where(side == 0, index - doc_start, lengths)
-    freq = 500000.0 ** (-jnp.arange(HD // 2, dtype=f32) * 2.0 / HD)
-    angle = positions.astype(f32)[:, None] * freq[None, :]
-    cosine, sine = jnp.cos(angle), jnp.sin(angle)
-    cosine = jnp.concatenate([cosine, cosine], axis=1)
-    sine = jnp.concatenate([-sine, sine], axis=1)
+    freq = np.float32(500000.0) ** (-np.arange(HD // 2, dtype=np.float32) * 2 / HD)
+    freq = jnp.asarray(np.concatenate([freq, freq])[None, :].astype(np.float32))
 
     half_block = jax.ShapeDtypeStruct((rows, width), bf16)
     query, fresh, arrived = pl.pallas_call(
-        functools.partial(gather_project, n),
-        out_shape=(half_block, jax.ShapeDtypeStruct((rows, 2 * HD), bf16),
-                   jax.ShapeDtypeStruct((rows, 2 * HD), bf16)),
-        in_specs=[in_vmem, anywhere, anywhere] + [in_vmem] * 5,
+        functools.partial(gather_project, page, n),
+        out_shape=(
+            half_block,
+            jax.ShapeDtypeStruct((rows, 2 * HD), bf16),
+            jax.ShapeDtypeStruct((rows, 2 * HD), bf16),
+        ),
+        in_specs=[in_smem] + [in_hbm] * 3 + [in_vmem] * 5,
         out_specs=(in_vmem, in_vmem, in_vmem),
         scratch_shapes=[
+            VMEM((rows, width), bf16),
             VMEM((n, rows, width), bf16),
             VMEM((n, 1, rows), f32),
             VMEM((rows, width + 2 * HD), f32),
@@ -461,50 +531,49 @@
             VMEM(q_words.shape, jnp.int32),
             VMEM(kv_words.shape[1:], jnp.int32),
             VMEM((rows, 2 * HD), bf16),
-            dma((2,)), sub_sems, sub_sems, dma((half,)), dma((half,)),
+            VMEM((rows, HD), f32),
+            VMEM((rows, HD), f32),
+            dma((3,)), gather_sems, gather_sems, dma((half,)), dma((half,)),
             dma, dma, dma((2,)),
         ],
         compiler_params=pltpu.CompilerParams(
-            collective_id=0, has_side_effects=True, vmem_limit_bytes=40 << 20
+            collective_id=0, has_side_effects=True, vmem_limit_bytes=GATHER_VMEM
         ),
         cost_estimate=pl.CostEstimate(
             flops=4 * n * rows * width * width, bytes_accessed=4 << 20, transcendentals=0
         ),
         name="gather_project",
     )(
-        x, q_words, kv_words[0], q_scales, kv_scales[0],
-        norm_gain.reshape(n, width), cosine, sine,
+        prompt_pages, x, q_words, kv_words[0], q_scales, kv_scales[0],
+        norm_gain.astype(f32).reshape(n, width), lengths.reshape(1, rows), freq,
     )
 
     def run_prefill():
         return pl.pallas_call(
-            prefill_kernel,
+            functools.partial(prefill_kernel, page),
             out_shape=half_block,
-            in_specs=[in_vmem] * 3,
+            in_specs=[in_smem] + [in_vmem] * 2,
             out_specs=in_vmem,
             name="prefill",
-        )(doc_start[:, None], query, fresh)
+        )(prompt_pages, query, fresh)
 
     def run_decode():
         span = block_tables.shape[1]
+        starts = jnp.cumsum(prompt_pages) - prompt_pages
         own = pool.shape[0] + jnp.minimum(
-            starts[:, None] // page + jnp.arange(span, dtype=jnp.int32)[None, :],
+            starts[:, None] + jnp.arange(span, dtype=jnp.int32)[None, :],
             page_slots.shape[0] - 1,
         )
         table = jnp.concatenate([own, block_tables], axis=0).reshape(-1)
         return pl.pallas_call(
             decode_kernel,
             out_shape=half_block,
-            in_specs=[pl.BlockSpec(memory_space=pltpu.SMEM)] + [in_vmem] * 4 + [anywhere],
+            in_specs=[in_smem] + [in_vmem] * 4 + [in_hbm],
             out_specs=in_vmem,
-            scratch_shapes=[
-                VMEM((pool.shape[0] + rows // page, page, 2 * HD), bf16),
-                VMEM((rows, width), f32),
-                VMEM((rows, 2 * HD), f32),
-                VMEM((rows, width), f32),
-                dma,
-            ],
-            compiler_params=pltpu.CompilerParams(vmem_limit_bytes=40 << 20),
+            scratch_shapes=decode_scratch(
+                rows, width, span * page, pool.shape[0] + rows // page, page
+            ),
+            compiler_params=pltpu.CompilerParams(vmem_limit_bytes=24 << 20),
             name="decode",
         )(table, lengths[:, None], query, fresh, arrived, pool)
 
@@ -513,16 +582,16 @@
     out = pl.pallas_call(
         functools.partial(project_scatter, n),
         out_shape=half_block,
-        in_specs=[in_vmem, anywhere, in_vmem],
+        in_specs=[in_vmem, in_hbm, in_vmem],
         out_specs=in_vmem,
         scratch_shapes=[
             VMEM((rows, width), bf16),
             VMEM(o_words.shape, jnp.int32),
             VMEM((2, width, width), bf16),
-            VMEM((2, rows, width), f32),
+            VMEM((2, 2, rows, width), f32),
             VMEM((rows, width), bf16),
             VMEM((n, rows, width), bf16),
-            dma, sub_sems, sub_sems, dma,
+            dma, scatter_sems, scatter_sems, dma,
         ],
         compiler_params=pltpu.CompilerParams(
             collective_id=1, has_side_effects=True, vmem_limit_bytes=40 << 20

time: 243 us -> 228 us (0.938)
  Pallas kernels: 232 us -> 223 us
  local copies, waits for them, and re-layouts: 7.5 us -> 2.55 us
    pallas_call x2, Pallas kernels: 171 us -> 149 us  [the longest x1 122 us: local(): pl.pallas_call(functools.partial(gather_project, page, n), out_shape=(hal...]
    pallas_call x1, Pallas kernels: 60.8 us -> 73.7 us  [local(): pl.pallas_call(functools.partial(project_scatter, n), out_shape=half_bloc...]
    unnamed x17 -> x9, local copies, waits for them, and re-layouts: 5.63 us -> 0.73 us
where the time goes in v2:
time: 228 us; the launch traced here: 227 us
  Pallas kernels  223 us (98%)
  local copies, waits for them, and re-layouts  2.55 us (1%)
    pallas_call x1, Pallas kernels, local(): pl.pallas_call(functools.partial(gather_project, page, n), out_shape=(hal...  122 us
    pallas_call x1, Pallas kernels, local(): pl.pallas_call(functools.partial(project_scatter, n), out_shape=half_bloc...  73.7 us
    pallas_call x1, Pallas kernels, run_decode(): pl.pallas_call(decode_kernel, out_shape=half_block, in_specs=[in_smem] +...  27.4 us

profile of v2, /device:TPU:37, one launch (start us, length us, event | category | flops | bytes accessed | tf_op | source)
XLA Modules:
  0.0 227.3 jit_solution(1787708236605563733)
XLA Ops:
  0.0 0.0 copy-start.3
  0.0 0.0 copy-start.2
  0.0 0.7 broadcast_multiply_fusion
  0.7 0.8 pad_add_fusion.1
  1.5 1.3 reshape.42.gain_ref
  2.8 121.6 %gather_project.1 = (bf16[512,256]{1,0:T(8,128)(2,1)S(1)}, bf16[512,256]{1,0:T(8,128)(2,1)S(1)}, bf16[512,256]{1,0:T(8,128)(2,1)S(1)}) custom-call(s32[16]{0:T(128)} %pages_ref.1, bf16[512,256]{1,0:T(8,128)(2,1)} %bitcast.14, s32[1024,256]{1,0:T(8,128)} %q_words.1, s32[1024,256]{1,0:T(8,128)} %bitcast.13, bf16[64,256]{1,0:T(8,128)(2,1)} %q_scales.1, ...), custom_call_target="tpu_custom_call" | custom-call | flops 4294967296 | bytes 4194304 | tf_op jit(solution)/shard_map/gather_project/pallas_call | solution.py:513
  124.4 0.0 copy-start
  124.4 0.0 copy-start.1
  124.4 0.0 copy-done.3
  124.4 0.0 copy-done.2
  124.4 28.4 %conditional.1 = (bf16[512,256]{1,0:T(8,128)(2,1)S(1)}) conditional(s32[]{:T(128)} %convert_element_type.4, (s32[16]{0:T(128)S(1)}, s32[496,16]{0,1:T(8,128)S(1)}, s32[512]{0:T(512)S(1)}, bf16[512,256]{1,0:T(8,128)(2,1)S(1)}, bf16[512,256]{1,0:T(8,128)(2,1)S(1)}, /*index=5*/bf16[512,256]{1,0:T(8,128)(2,1)S(1)}, ...), branch_computations={%region_0.2_spmd, %region_2.3_spmd} | conditional | flops 9216 | bytes 202384 | solution.py:580
  124.4 0.1 copy.20
  124.6 0.1 reduce
  124.7 0.1 pad_add_fusion
  124.8 0.1 copy.21
  124.9 0.1 reshape.34.table_ref
  125.1 0.1 copy.22.length_ref
  125.2 27.4 %decode.1 = bf16[512,256]{1,0:T(8,128)(2,1)S(1)} custom-call(s32[8192]{0:T(1024)S(1)} %reshape.34.table_ref, s32[512,1]{1,0:T(8,128)S(1)} %copy.22.length_ref, bf16[512,256]{1,0:T(8,128)(2,1)S(1)} %get-tuple-element.31.q_ref, bf16[512,256]{1,0:T(8,128)(2,1)S(1)} %get-tuple-element.32.kv_ref, bf16[512,256]{1,0:T(8,128)(2,1)S(1)} %get-tuple-element.33.fresh_ref, ...), custom_call_target="tpu_custom_call" | custom-call | tf_op jit(solution)/shard_map/cond/branch_0_fun/decode/pallas_call | solution.py:568
  152.8 0.0 copy-done
  152.9 0.0 copy-done.1
  152.9 73.7 %project_scatter.1 = bf16[512,256]{1,0:T(8,128)(2,1)S(1)} custom-call(bf16[512,256]{1,0:T(8,128)(2,1)S(1)} %get-tuple-element.56.att_ref, s32[32,8192]{1,0:T(8,128)S(1)} %copy-done, bf16[2,8192]{1,0:T(2,128)(2,1)S(1)} %copy-done.1), custom_call_target="tpu_custom_call" | custom-call | flops 2147483648 | bytes 4194304 | tf_op jit(solution)/shard_map/project_scatter/pallas_call | solution.py:582
  226.6 0.7 copy.26
  (3 shorter events, 0.1 us)
Async XLA Ops:
  0.0 124.4 %copy-start.3 = (s32[16]{0:T(128)S(1)}, s32[16]{0:T(128)}, u32[]{:S(2)}) copy-start(s32[16]{0:T(128)} %pages_ref.1) | copy-start | bytes 196
  0.0 124.4 %copy-start.2 = (s32[496,16]{0,1:T(8,128)S(1)}, s32[496,16]{0,1:T(8,128)}, u32[]{:S(2)}) copy-start(s32[496,16]{0,1:T(8,128)} %param.26) | copy-start | bytes 95236
  124.4 28.5 %copy-start = (s32[32,8192]{1,0:T(8,128)S(1)}, s32[32,8192]{1,0:T(8,128)}, u32[]{:S(2)}) copy-start(s32[32,8192]{1,0:T(8,128)} %o_words.1) | copy-start | bytes 3145732
  124.4 28.5 %copy-start.1 = (bf16[2,8192]{1,0:T(2,128)(2,1)S(1)}, bf16[2,8192]{1,0:T(2,128)(2,1)}, u32[]{:S(2)}) copy-start(bf16[2,8192]{1,0:T(2,128)(2,1)} %scale_ref.1) | copy-start | bytes 98308

commit v3 on v2

--- a/solution.py
+++ b/solution.py
@@ -10,8 +10,8 @@
 
 HD = 128
 LONGEST = 128
-GATHER_PIECES = 4
-SCATTER_PIECES = 8
+GATHER_PIECES = 8
+SCATTER_PIECES = 16
 GATHER_VMEM = 58 << 20
 MESH = pl.DeviceIdType.MESH
 VMEM = pltpu.VMEM
@@ -63,9 +63,9 @@
 
 
 def gather_project(
-    page, n, pages_ref, x_hbm, q_words, kv_words, q_scales, kv_scales, gain_ref,
-    length_ref, freq_ref, q_out, kv_out, fresh_out,
-    x_ref, xbuf, stat, acc, weights, inverse, gains, scales, qw, kw, arrived, cosine, sine,
+    page, n, pages_ref, length_ref, x_hbm, q_words, kv_words, q_scales, kv_scales, gain_ref,
+    freq_ref, q_out, kv_out, fresh_out,
+    x_ref, xbuf, stat, acc, weights, inverse, gains, scales, qw, kw, arrived, cosine, sine, held,
     load_sem, recv_right, recv_left, stat_right, stat_left, send_sem, stat_send, pair_sem,
 ):
     me, right, left = ring(n)
@@ -159,15 +159,27 @@
         data(me, 0, u, True).start()
         data(me, 0, u, False).start()
     gains[...] = jnp.dot(
-        gain_ref[...].astype(jnp.bfloat16), order, preferred_element_type=jnp.float32
+        gain_ref[...], order, preferred_element_type=jnp.float32
     )
     scales[:, 0:width] = q_scales[...].astype(jnp.float32)
     scales[:, width:] = kv_scales[...].astype(jnp.float32)
     acc[...] = jnp.zeros_like(acc)
     row = lax.broadcasted_iota(jnp.int32, (rows, HD), 0)
     placed = (row - prompt_start(pages_ref, page, row)).astype(jnp.float32)
-    held = jnp.broadcast_to(length_ref[...].astype(jnp.float32), (HD, rows)).T
-    angle = jnp.where(role == 0, placed, held) * freq_ref[...]
+    prompts = pages_ref.shape[0]
+    line = lax.broadcasted_iota(jnp.int32, (8, HD), 0)
+
+    @pl.loop(0, rows // 8)
+    def _(b):
+        block = jnp.zeros((8, HD), jnp.int32)
+        for t in range(8):
+            i = 8 * b + t
+            whole = pages_ref[jnp.minimum(i, prompts - 1)] * page
+            length = jnp.where(i < prompts, whole, length_ref[jnp.maximum(i - prompts, 0)])
+            block = jnp.where(line == t, length, block)
+        held[pl.ds(pl.multiple_of(8 * b, 8), 8), :] = block.astype(jnp.float32)
+
+    angle = jnp.where(role == 0, placed, held[...]) * freq_ref[...]
     cosine[...] = jnp.cos(angle)
     turned = jnp.sin(angle)
     lane = lax.broadcasted_iota(jnp.int32, (rows, HD), 1)
@@ -258,8 +270,8 @@
 
 
 def project_scatter(
-    n, att_ref, o_words, scale_ref, out_ref,
-    attended, ow, weights, part, begun, slots, load_sem, recv_right, recv_left, send_sem,
+    n, att_ref, ow, scale_ref, out_ref,
+    attended, weights, part, begun, slots, recv_right, recv_left, send_sem,
 ):
     me, right, left = ring(n)
     half = n // 2
@@ -267,12 +279,9 @@
     pieces = recv_right.shape[1]
     sub = rows // pieces
     barrier = signal_ready(({"tp": right}, {"tp": left}))
-    load = pltpu.make_async_copy(o_words, ow, load_sem)
-    load.start()
     attended[...] = jnp.dot(
         att_ref[...], nibble_order(width), preferred_element_type=jnp.float32
     ).astype(jnp.bfloat16)
-    load.wait()
 
     def unpack(side, dest):
         columns = pl.ds(pl.multiple_of(dest * width, width), width)
@@ -505,7 +514,6 @@
     in_hbm = pl.BlockSpec(memory_space=pltpu.HBM)
     bf16, f32 = jnp.bfloat16, jnp.float32
 
-    lengths = jnp.concatenate([prompt_pages * page, cache_lens])
     freq = np.float32(500000.0) ** (-np.arange(HD // 2, dtype=np.float32) * 2 / HD)
     freq = jnp.asarray(np.concatenate([freq, freq])[None, :].astype(np.float32))
 
@@ -517,7 +525,7 @@
             jax.ShapeDtypeStruct((rows, 2 * HD), bf16),
             jax.ShapeDtypeStruct((rows, 2 * HD), bf16),
         ),
-        in_specs=[in_smem] + [in_hbm] * 3 + [in_vmem] * 5,
+        in_specs=[in_smem] * 2 + [in_hbm] * 3 + [in_vmem] * 4,
         out_specs=(in_vmem, in_vmem, in_vmem),
         scratch_shapes=[
             VMEM((rows, width), bf16),
@@ -533,6 +541,7 @@
             VMEM((rows, 2 * HD), bf16),
             VMEM((rows, HD), f32),
             VMEM((rows, HD), f32),
+            VMEM((rows, HD), f32),
             dma((3,)), gather_sems, gather_sems, dma((half,)), dma((half,)),
             dma, dma, dma((2,)),
         ],
@@ -544,8 +553,8 @@
         ),
         name="gather_project",
     )(
-        prompt_pages, x, q_words, kv_words[0], q_scales, kv_scales[0],
-        norm_gain.astype(f32).reshape(n, width), lengths.reshape(1, rows), freq,
+        prompt_pages, cache_lens, x, q_words, kv_words[0], q_scales, kv_scales[0],
+        norm_gain.reshape(n, width), freq,
     )
 
     def run_prefill():
@@ -560,6 +569,7 @@
     def run_decode():
         span = block_tables.shape[1]
         starts = jnp.cumsum(prompt_pages) - prompt_pages
+        lengths = jnp.concatenate([prompt_pages * page, cache_lens])
         own = pool.shape[0] + jnp.minimum(
             starts[:, None] + jnp.arange(span, dtype=jnp.int32)[None, :],
             page_slots.shape[0] - 1,
@@ -582,16 +592,15 @@
     out = pl.pallas_call(
         functools.partial(project_scatter, n),
         out_shape=half_block,
-        in_specs=[in_vmem, in_hbm, in_vmem],
+        in_specs=[in_vmem] * 3,
         out_specs=in_vmem,
         scratch_shapes=[
             VMEM((rows, width), bf16),
-            VMEM(o_words.shape, jnp.int32),
             VMEM((2, width, width), bf16),
             VMEM((2, 2, rows, width), f32),
             VMEM((rows, width), bf16),
             VMEM((n, rows, width), bf16),
-            dma, scatter_sems, scatter_sems, dma,
+            scatter_sems, scatter_sems, dma,
         ],
         compiler_params=pltpu.CompilerParams(
             collective_id=1, has_side_effects=True, vmem_limit_bytes=40 << 20

time: 228 us -> 228 us (level)
  no operation moved by 1% of the time
where the time goes in v3:
time: 228 us
  Pallas kernels  225 us (99%)
  local copies, waits for them, and re-layouts  2.58 us (1%)
    pallas_call x1, Pallas kernels, local(): pl.pallas_call(functools.partial(gather_project, page, n), out_shape=(hal...  122 us
    pallas_call x1, Pallas kernels, local(): pl.pallas_call(functools.partial(project_scatter, n), out_shape=half_bloc...  75.3 us
    pallas_call x1, Pallas kernels, run_decode(): pl.pallas_call(decode_kernel, out_shape=half_block, in_specs=[in_smem] +...  27.4 us

profile of v3, /device:TPU:37, one launch (start us, length us, event | category | flops | bytes accessed | tf_op | source)
XLA Modules:
  0.0 228.0 jit_solution(1142722498898999528)
XLA Ops:
  0.0 0.0 copy-start.3
  0.0 0.0 copy-start.4
  0.0 0.0 copy-start.2
  0.0 1.4 reshape.33.gain_ref
  1.4 122.0 %gather_project.1 = (bf16[512,256]{1,0:T(8,128)(2,1)S(1)}, bf16[512,256]{1,0:T(8,128)(2,1)S(1)}, bf16[512,256]{1,0:T(8,128)(2,1)S(1)}) custom-call(s32[16]{0:T(128)} %pages_ref.1, s32[496]{0:T(512)} %length_ref.1, bf16[512,256]{1,0:T(8,128)(2,1)} %bitcast.12, s32[1024,256]{1,0:T(8,128)} %q_words.1, s32[1024,256]{1,0:T(8,128)} %bitcast.11, ...), custom_call_target="tpu_custom_call" | custom-call | flops 4294967296 | bytes 4194304 | tf_op jit(solution)/shard_map/gather_project/pallas_call | solution.py:521
  123.4 0.0 copy-start
  123.4 0.0 copy-start.1
  123.4 0.0 copy-done.3
  123.4 0.0 copy-done.4
  123.4 0.0 copy-done.2
  123.5 28.5 %conditional.1 = (bf16[512,256]{1,0:T(8,128)(2,1)S(1)}) conditional(s32[]{:T(128)} %convert_element_type.3, (s32[16]{0:T(128)S(1)}, s32[496,16]{0,1:T(8,128)S(1)}, s32[496]{0:T(512)S(1)}, bf16[512,256]{1,0:T(8,128)(2,1)S(1)}, bf16[512,256]{1,0:T(8,128)(2,1)S(1)}, /*index=5*/bf16[512,256]{1,0:T(8,128)(2,1)S(1)}, ...), branch_computations={%region_0.2_spmd, %region_2.3_spmd} | conditional | flops 9744 | bytes 206544 | solution.py:590
  123.5 0.1 copy.20
  123.6 0.1 reduce
  123.7 0.1 pad_add_fusion.1
  123.8 0.1 pad_add_fusion
  123.9 0.1 copy.21
  124.0 0.1 reshape.31.table_ref
  124.2 0.1 copy.22.length_ref
  124.3 27.4 %decode.1 = bf16[512,256]{1,0:T(8,128)(2,1)S(1)} custom-call(s32[8192]{0:T(1024)S(1)} %reshape.31.table_ref, s32[512,1]{1,0:T(8,128)S(1)} %copy.22.length_ref, bf16[512,256]{1,0:T(8,128)(2,1)S(1)} %get-tuple-element.31.q_ref, bf16[512,256]{1,0:T(8,128)(2,1)S(1)} %get-tuple-element.32.kv_ref, bf16[512,256]{1,0:T(8,128)(2,1)S(1)} %get-tuple-element.33.fresh_ref, ...), custom_call_target="tpu_custom_call" | custom-call | tf_op jit(solution)/shard_map/cond/branch_0_fun/decode/pallas_call | solution.py:578
  151.9 0.0 copy-done
  152.0 0.0 copy-done.1
  152.0 75.3 %project_scatter.1 = bf16[512,256]{1,0:T(8,128)(2,1)S(1)} custom-call(bf16[512,256]{1,0:T(8,128)(2,1)S(1)} %get-tuple-element.58.att_ref, s32[32,8192]{1,0:T(8,128)S(1)} %copy-done, bf16[2,8192]{1,0:T(2,128)(2,1)S(1)} %copy-done.1), custom_call_target="tpu_custom_call" | custom-call | flops 2147483648 | bytes 4194304 | tf_op jit(solution)/shard_map/project_scatter/pallas_call | solution.py:592
  227.3 0.7 copy.26
  (3 shorter events, 0.1 us)
Async XLA Ops:
  0.0 123.4 %copy-start.3 = (s32[16]{0:T(128)S(1)}, s32[16]{0:T(128)}, u32[]{:S(2)}) copy-start(s32[16]{0:T(128)} %pages_ref.1) | copy-start | bytes 196
  0.0 123.4 %copy-start.4 = (s32[496]{0:T(512)S(1)}, s32[496]{0:T(512)}, u32[]{:S(2)}) copy-start(s32[496]{0:T(512)} %length_ref.1) | copy-start | bytes 5956
  0.0 123.4 %copy-start.2 = (s32[496,16]{0,1:T(8,128)S(1)}, s32[496,16]{0,1:T(8,128)}, u32[]{:S(2)}) copy-start(s32[496,16]{0,1:T(8,128)} %param.26) | copy-start | bytes 95236
  123.4 28.5 %copy-start = (s32[32,8192]{1,0:T(8,128)S(1)}, s32[32,8192]{1,0:T(8,128)}, u32[]{:S(2)}) copy-start(s32[32,8192]{1,0:T(8,128)} %ow.1) | copy-start | bytes 3145732
  123.4 28.5 %copy-start.1 = (bf16[2,8192]{1,0:T(2,128)(2,1)S(1)}, bf16[2,8192]{1,0:T(2,128)(2,1)}, u32[]{:S(2)}) copy-start(bf16[2,8192]{1,0:T(2,128)(2,1)} %scale_ref.1) | copy-start | bytes 98308

commit v4 on v3

--- a/solution.py
+++ b/solution.py
@@ -10,8 +10,9 @@
 
 HD = 128
 LONGEST = 128
-GATHER_PIECES = 8
-SCATTER_PIECES = 16
+GATHER_PIECES = 4
+SCATTER_PIECES = 8
+LEAD = 4
 GATHER_VMEM = 58 << 20
 MESH = pl.DeviceIdType.MESH
 VMEM = pltpu.VMEM
@@ -66,7 +67,7 @@
     page, n, pages_ref, length_ref, x_hbm, q_words, kv_words, q_scales, kv_scales, gain_ref,
     freq_ref, q_out, kv_out, fresh_out,
     x_ref, xbuf, stat, acc, weights, inverse, gains, scales, qw, kw, arrived, cosine, sine, held,
-    load_sem, recv_right, recv_left, stat_right, stat_left, send_sem, stat_send, pair_sem,
+    load_sem, recv_right, recv_left, stat_right, stat_left, send_sem, stat_send, pair_sem, lead_sem,
 ):
     me, right, left = ring(n)
     role = lax.axis_index("role")
@@ -153,13 +154,20 @@
             acc[part, :] += jnp.dot(normed, weights[...], preferred_element_type=jnp.float32)
 
     pl.semaphore_wait(barrier, 3)
+
+    @pl.when(role == 1)
+    def _():
+        pl.semaphore_wait(lead_sem, 1)
+
     figure(me, 0, True).start()
     figure(me, 0, False).start()
     for u in range(pieces):
         data(me, 0, u, True).start()
         data(me, 0, u, False).start()
+    for i in range(n):
+        gains[i : i + 1, :] = gain_ref[i * width : (i + 1) * width].astype(jnp.float32)[None, :]
     gains[...] = jnp.dot(
-        gain_ref[...], order, preferred_element_type=jnp.float32
+        gains[...].astype(jnp.bfloat16), order, preferred_element_type=jnp.float32
     )
     scales[:, 0:width] = q_scales[...].astype(jnp.float32)
     scales[:, width:] = kv_scales[...].astype(jnp.float32)
@@ -192,6 +200,12 @@
 
     @pl.loop(1, turn)
     def _(s):
+        @pl.when((role == 0) & (s == min(LEAD, turn - 1)))
+        def _():
+            pl.semaphore_signal(
+                lead_sem, inc=1, device_id={"role": 1 - role}, device_id_type=MESH
+            )
+
         for u in range(pieces):
             pass_data(s, u)
             if u == 2 * quarter - 1:
@@ -543,7 +557,7 @@
             VMEM((rows, HD), f32),
             VMEM((rows, HD), f32),
             dma((3,)), gather_sems, gather_sems, dma((half,)), dma((half,)),
-            dma, dma, dma((2,)),
+            dma, dma, dma((2,)), pltpu.SemaphoreType.REGULAR,
         ],
         compiler_params=pltpu.CompilerParams(
             collective_id=0, has_side_effects=True, vmem_limit_bytes=GATHER_VMEM
@@ -554,7 +568,7 @@
         name="gather_project",
     )(
         prompt_pages, cache_lens, x, q_words, kv_words[0], q_scales, kv_scales[0],
-        norm_gain.reshape(n, width), freq,
+        norm_gain, freq,
     )
 
     def run_prefill():

time: 228 us -> 226 us (level)
    pallas_call x1, Pallas kernels: 75.3 us -> 66.7 us  [local(): pl.pallas_call(functools.partial(project_scatter, n), out_shape=half_bloc...]
    pallas_call x1, Pallas kernels: 122 us -> 129 us  [local(): pl.pallas_call(functools.partial(gather_project, page, n), out_shape=(hal...]
where the time goes in v4:
time: 226 us; the launch traced here: 225 us
  Pallas kernels  223 us (99%)
    pallas_call x1, Pallas kernels, local(): pl.pallas_call(functools.partial(gather_project, page, n), out_shape=(hal...  129 us
    pallas_call x1, Pallas kernels, local(): pl.pallas_call(functools.partial(project_scatter, n), out_shape=half_bloc...  66.7 us
    pallas_call x1, Pallas kernels, run_decode(): pl.pallas_call(decode_kernel, out_shape=half_block, in_specs=[in_smem] +...  27.4 us

profile of v4, /device:TPU:37, one launch (start us, length us, event | category | flops | bytes accessed | tf_op | source)
XLA Modules:
  0.0 225.4 jit_solution(11118917112034073354)
XLA Ops:
  0.0 0.0 copy-start.3
  0.0 0.0 copy-start.4
  0.0 0.0 copy-start.2
  0.0 129.4 %gather_project.1 = (bf16[512,256]{1,0:T(8,128)(2,1)S(1)}, bf16[512,256]{1,0:T(8,128)(2,1)S(1)}, bf16[512,256]{1,0:T(8,128)(2,1)S(1)}) custom-call(s32[16]{0:T(128)} %pages_ref.1, s32[496]{0:T(512)} %length_ref.1, bf16[512,256]{1,0:T(8,128)(2,1)} %bitcast.12, s32[1024,256]{1,0:T(8,128)} %q_words.1, s32[1024,256]{1,0:T(8,128)} %bitcast.11, ...), custom_call_target="tpu_custom_call" | custom-call | flops 4294967296 | bytes 4194304 | tf_op jit(solution)/shard_map/gather_project/pallas_call | solution.py:535
  129.4 0.0 copy-start
  129.4 0.0 copy-start.1
  129.4 0.0 copy-done.3
  129.4 0.0 copy-done.4
  129.4 0.0 copy-done.2
  129.4 28.5 %conditional.1 = (bf16[512,256]{1,0:T(8,128)(2,1)S(1)}) conditional(s32[]{:T(128)} %convert_element_type.3, (s32[16]{0:T(128)S(1)}, s32[496,16]{0,1:T(8,128)S(1)}, s32[496]{0:T(512)S(1)}, bf16[512,256]{1,0:T(8,128)(2,1)S(1)}, bf16[512,256]{1,0:T(8,128)(2,1)S(1)}, /*index=5*/bf16[512,256]{1,0:T(8,128)(2,1)S(1)}, ...), branch_computations={%region_0.2_spmd, %region_2.3_spmd} | conditional | flops 9744 | bytes 206544 | solution.py:604
  129.5 0.1 copy.20
  129.6 0.1 reduce
  129.7 0.1 pad_add_fusion.1
  129.8 0.1 pad_add_fusion
  129.9 0.1 copy.21
  130.0 0.1 reshape.29.table_ref
  130.1 0.1 copy.22.length_ref
  130.3 27.4 %decode.1 = bf16[512,256]{1,0:T(8,128)(2,1)S(1)} custom-call(s32[8192]{0:T(1024)S(1)} %reshape.29.table_ref, s32[512,1]{1,0:T(8,128)S(1)} %copy.22.length_ref, bf16[512,256]{1,0:T(8,128)(2,1)S(1)} %get-tuple-element.31.q_ref, bf16[512,256]{1,0:T(8,128)(2,1)S(1)} %get-tuple-element.32.kv_ref, bf16[512,256]{1,0:T(8,128)(2,1)S(1)} %get-tuple-element.33.fresh_ref, ...), custom_call_target="tpu_custom_call" | custom-call | tf_op jit(solution)/shard_map/cond/branch_0_fun/decode/pallas_call | solution.py:592
  157.9 0.0 copy-done
  157.9 0.0 copy-done.1
  157.9 66.7 %project_scatter.1 = bf16[512,256]{1,0:T(8,128)(2,1)S(1)} custom-call(bf16[512,256]{1,0:T(8,128)(2,1)S(1)} %get-tuple-element.58.att_ref, s32[32,8192]{1,0:T(8,128)S(1)} %copy-done, bf16[2,8192]{1,0:T(2,128)(2,1)S(1)} %copy-done.1), custom_call_target="tpu_custom_call" | custom-call | flops 2147483648 | bytes 4194304 | tf_op jit(solution)/shard_map/project_scatter/pallas_call | solution.py:606
  224.7 0.7 copy.26
  (3 shorter events, 0.1 us)
Async XLA Ops:
  0.0 129.4 %copy-start.3 = (s32[16]{0:T(128)S(1)}, s32[16]{0:T(128)}, u32[]{:S(2)}) copy-start(s32[16]{0:T(128)} %pages_ref.1) | copy-start | bytes 196
  0.0 129.4 %copy-start.4 = (s32[496]{0:T(512)S(1)}, s32[496]{0:T(512)}, u32[]{:S(2)}) copy-start(s32[496]{0:T(512)} %length_ref.1) | copy-start | bytes 5956
  0.0 129.4 %copy-start.2 = (s32[496,16]{0,1:T(8,128)S(1)}, s32[496,16]{0,1:T(8,128)}, u32[]{:S(2)}) copy-start(s32[496,16]{0,1:T(8,128)} %param.26) | copy-start | bytes 95236
  129.4 28.5 %copy-start = (s32[32,8192]{1,0:T(8,128)S(1)}, s32[32,8192]{1,0:T(8,128)}, u32[]{:S(2)}) copy-start(s32[32,8192]{1,0:T(8,128)} %ow.1) | copy-start | bytes 3145732
  129.4 28.5 %copy-start.1 = (bf16[2,8192]{1,0:T(2,128)(2,1)S(1)}, bf16[2,8192]{1,0:T(2,128)(2,1)}, u32[]{:S(2)}) copy-start(bf16[2,8192]{1,0:T(2,128)(2,1)} %scale_ref.1) | copy-start | bytes 98308

commit v5 on v4

--- a/solution.py
+++ b/solution.py
@@ -12,6 +12,7 @@
 LONGEST = 128
 GATHER_PIECES = 4
 SCATTER_PIECES = 8
+REACH = 4
 LEAD = 4
 GATHER_VMEM = 58 << 20
 MESH = pl.DeviceIdType.MESH
@@ -76,7 +77,17 @@
     pieces = recv_right.shape[1]
     sub = rows // pieces
 
-    barrier = signal_ready(({"tp": right}, {"tp": left}, {"role": 1 - role}))
+    reach = min(REACH, half)
+    groups = half // reach
+
+    def behind(s):
+        return lax.rem(me + n - s, n)
+
+    def ahead(s):
+        return lax.rem(me + s, n)
+
+    peers = [{"tp": side(d)} for d in range(1, reach + 1) for side in (ahead, behind)]
+    barrier = signal_ready(peers + [{"role": 1 - role}])
     load_x = pltpu.make_async_copy(x_hbm, x_ref, load_sem.at[0])
     loads = (
         pltpu.make_async_copy(q_words, qw, load_sem.at[1]),
@@ -108,27 +119,33 @@
             device_id_type=MESH,
         )
 
-    def figure(chunk, hop, to_right):
+    def figure(chunk, sem, peer):
         return pltpu.make_async_remote_copy(
             src_ref=stat.at[chunk],
             dst_ref=stat.at[chunk],
             send_sem=stat_send,
-            recv_sem=(stat_right if to_right else stat_left).at[hop],
-            device_id={"tp": right if to_right else left},
+            recv_sem=sem,
+            device_id={"tp": peer},
             device_id_type=MESH,
         )
 
-    def behind(s):
-        return lax.rem(me + n - s, n)
-
-    def ahead(s):
-        return lax.rem(me + s, n)
-
-    def pass_figures(h):
-        figure(behind(h), h - 1, True).wait_recv()
-        figure(behind(h), h, True).start()
-        figure(ahead(h), h - 1, False).wait_recv()
-        figure(ahead(h), h, False).start()
+    def take_figures(g):
+        for d in range(1, reach + 1):
+            k = reach * (g - 1) + d
+            figure(behind(k), stat_right.at[k - 1], right).wait_recv()
+
+            @pl.when(k < half)
+            def _():
+                figure(ahead(k), stat_left.at[k - 1], left).wait_recv()
+
+    def hand_on_figures(g):
+        for d in range(1, reach + 1):
+            k = reach * (g - 1) + d
+            figure(behind(k), stat_right.at[k + reach - 1], ahead(reach)).start()
+
+            @pl.when(k + reach < half)
+            def _():
+                figure(ahead(k), stat_left.at[k + reach - 1], behind(reach)).start()
 
     def pass_data(s, u):
         data(behind(s), s - 1, u, True).wait_recv()
@@ -153,14 +170,16 @@
             normed = (xbuf[chunk, part, :].astype(jnp.float32) * scale * gain).astype(jnp.bfloat16)
             acc[part, :] += jnp.dot(normed, weights[...], preferred_element_type=jnp.float32)
 
-    pl.semaphore_wait(barrier, 3)
+    pl.semaphore_wait(barrier, 2 * reach + 1)
 
     @pl.when(role == 1)
     def _():
         pl.semaphore_wait(lead_sem, 1)
 
-    figure(me, 0, True).start()
-    figure(me, 0, False).start()
+    for d in range(1, reach + 1):
+        figure(me, stat_right.at[d - 1], ahead(d)).start()
+        if d < half:
+            figure(me, stat_left.at[d - 1], behind(d)).start()
     for u in range(pieces):
         data(me, 0, u, True).start()
         data(me, 0, u, False).start()
@@ -194,7 +213,6 @@
     sine[...] = jnp.where(lane < HD // 2, -turned, turned)
     for load in loads:
         load.wait()
-    pass_figures(1)
 
     quarter = pieces // 4
 
@@ -208,21 +226,14 @@
 
         for u in range(pieces):
             pass_data(s, u)
-            if u == 2 * quarter - 1:
-                pass_figures(2 * s)
-            if u == pieces - 1:
-
-                @pl.when(2 * s + 1 < half - 1)
-                def _():
-                    pass_figures(2 * s + 1)
-
-                @pl.when(2 * s + 1 == half - 1)
-                def _():
-                    figure(behind(half - 1), half - 2, True).wait_recv()
-                    figure(behind(half - 1), half - 1, True).start()
-                    figure(ahead(half - 1), half - 2, False).wait_recv()
-
-    figure(behind(half), half - 1, True).wait_recv()
+        group = (s + 1) // 2
+
+        @pl.when((lax.rem(s, 2) == 1) & (group < groups))
+        def _():
+            take_figures(group)
+            hand_on_figures(group)
+
+    take_figures(groups)
     total = stat[0]
     for i in range(1, n):
         total = total + stat[i]

time: 226 us -> 220 us (0.973)
  Pallas kernels: 223 us -> 218 us
    pallas_call x1, Pallas kernels: 129 us -> 125 us  [local(): pl.pallas_call(functools.partial(gather_project, page, n), out_shape=(hal...]
where the time goes in v5:
time: 220 us
  Pallas kernels  218 us (99%)
    pallas_call x1, Pallas kernels, local(): pl.pallas_call(functools.partial(gather_project, page, n), out_shape=(hal...  125 us
    pallas_call x1, Pallas kernels, local(): pl.pallas_call(functools.partial(project_scatter, n), out_shape=half_bloc...  65.2 us
    pallas_call x1, Pallas kernels, run_decode(): pl.pallas_call(decode_kernel, out_shape=half_block, in_specs=[in_smem] +...  27.4 us

profile of v5, /device:TPU:37, one launch (start us, length us, event | category | flops | bytes accessed | tf_op | source)
XLA Modules:
  0.0 219.5 jit_solution(12577876281468020386)
XLA Ops:
  0.0 0.0 copy-start.3
  0.0 0.0 copy-start.4
  0.0 0.0 copy-start.2
  0.0 125.0 %gather_project.1 = (bf16[512,256]{1,0:T(8,128)(2,1)S(1)}, bf16[512,256]{1,0:T(8,128)(2,1)S(1)}, bf16[512,256]{1,0:T(8,128)(2,1)S(1)}) custom-call(s32[16]{0:T(128)} %pages_ref.1, s32[496]{0:T(512)} %length_ref.1, bf16[512,256]{1,0:T(8,128)(2,1)} %bitcast.12, s32[1024,256]{1,0:T(8,128)} %q_words.1, s32[1024,256]{1,0:T(8,128)} %bitcast.11, ...), custom_call_target="tpu_custom_call" | custom-call | flops 4294967296 | bytes 4194304 | tf_op jit(solution)/shard_map/gather_project/pallas_call | solution.py:546
  125.0 0.0 copy-start
  125.1 0.0 copy-start.1
  125.1 0.0 copy-done.3
  125.1 0.0 copy-done.4
  125.1 0.0 copy-done.2
  125.1 28.5 %conditional.1 = (bf16[512,256]{1,0:T(8,128)(2,1)S(1)}) conditional(s32[]{:T(128)} %convert_element_type.3, (s32[16]{0:T(128)S(1)}, s32[496,16]{0,1:T(8,128)S(1)}, s32[496]{0:T(512)S(1)}, bf16[512,256]{1,0:T(8,128)(2,1)S(1)}, bf16[512,256]{1,0:T(8,128)(2,1)S(1)}, /*index=5*/bf16[512,256]{1,0:T(8,128)(2,1)S(1)}, ...), branch_computations={%region_0.2_spmd, %region_2.3_spmd} | conditional | flops 9744 | bytes 206544 | solution.py:615
  125.1 0.1 copy.20
  125.2 0.1 reduce
  125.4 0.1 pad_add_fusion.1
  125.5 0.1 pad_add_fusion
  125.5 0.1 copy.21
  125.7 0.1 reshape.29.table_ref
  125.8 0.1 copy.22.length_ref
  126.0 27.4 %decode.1 = bf16[512,256]{1,0:T(8,128)(2,1)S(1)} custom-call(s32[8192]{0:T(1024)S(1)} %reshape.29.table_ref, s32[512,1]{1,0:T(8,128)S(1)} %copy.22.length_ref, bf16[512,256]{1,0:T(8,128)(2,1)S(1)} %get-tuple-element.31.q_ref, bf16[512,256]{1,0:T(8,128)(2,1)S(1)} %get-tuple-element.32.kv_ref, bf16[512,256]{1,0:T(8,128)(2,1)S(1)} %get-tuple-element.33.fresh_ref, ...), custom_call_target="tpu_custom_call" | custom-call | tf_op jit(solution)/shard_map/cond/branch_0_fun/decode/pallas_call | solution.py:603
  153.6 0.0 copy-done
  153.6 0.0 copy-done.1
  153.6 65.2 %project_scatter.1 = bf16[512,256]{1,0:T(8,128)(2,1)S(1)} custom-call(bf16[512,256]{1,0:T(8,128)(2,1)S(1)} %get-tuple-element.58.att_ref, s32[32,8192]{1,0:T(8,128)S(1)} %copy-done, bf16[2,8192]{1,0:T(2,128)(2,1)S(1)} %copy-done.1), custom_call_target="tpu_custom_call" | custom-call | flops 2147483648 | bytes 4194304 | tf_op jit(solution)/shard_map/project_scatter/pallas_call | solution.py:617
  218.8 0.7 copy.26
  (3 shorter events, 0.1 us)
Async XLA Ops:
  0.0 125.1 %copy-start.3 = (s32[16]{0:T(128)S(1)}, s32[16]{0:T(128)}, u32[]{:S(2)}) copy-start(s32[16]{0:T(128)} %pages_ref.1) | copy-start | bytes 196
  0.0 125.1 %copy-start.4 = (s32[496]{0:T(512)S(1)}, s32[496]{0:T(512)}, u32[]{:S(2)}) copy-start(s32[496]{0:T(512)} %length_ref.1) | copy-start | bytes 5956
  0.0 125.1 %copy-start.2 = (s32[496,16]{0,1:T(8,128)S(1)}, s32[496,16]{0,1:T(8,128)}, u32[]{:S(2)}) copy-start(s32[496,16]{0,1:T(8,128)} %param.26) | copy-start | bytes 95236
  125.0 28.5 %copy-start = (s32[32,8192]{1,0:T(8,128)S(1)}, s32[32,8192]{1,0:T(8,128)}, u32[]{:S(2)}) copy-start(s32[32,8192]{1,0:T(8,128)} %ow.1) | copy-start | bytes 3145732
  125.1 28.5 %copy-start.1 = (bf16[2,8192]{1,0:T(2,128)(2,1)S(1)}, bf16[2,8192]{1,0:T(2,128)(2,1)}, u32[]{:S(2)}) copy-start(bf16[2,8192]{1,0:T(2,128)(2,1)} %scale_ref.1) | copy-start | bytes 98308

commit v6 on v5

--- a/solution.py
+++ b/solution.py
@@ -11,7 +11,7 @@
 HD = 128
 LONGEST = 128
 GATHER_PIECES = 4
-SCATTER_PIECES = 8
+SCATTER_PIECES = 4
 REACH = 4
 LEAD = 4
 GATHER_VMEM = 58 << 20

time: 220 us -> 220 us (level)
  no operation moved by 1% of the time
where the time goes in v6:
time: 220 us
  Pallas kernels  218 us (99%)
    pallas_call x1, Pallas kernels, local(): pl.pallas_call(functools.partial(gather_project, page, n), out_shape=(hal...  125 us
    pallas_call x1, Pallas kernels, local(): pl.pallas_call(functools.partial(project_scatter, n), out_shape=half_bloc...  65.9 us
    pallas_call x1, Pallas kernels, run_decode(): pl.pallas_call(decode_kernel, out_shape=half_block, in_specs=[in_smem] +...  27.4 us

profile of v6, /device:TPU:37, one launch (start us, length us, event | category | flops | bytes accessed | tf_op | source)
XLA Modules:
  0.0 220.2 jit_solution(11217755553984884458)
XLA Ops:
  0.0 0.0 copy-start.3
  0.0 0.0 copy-start.4
  0.0 0.0 copy-start.2
  0.0 125.0 %gather_project.1 = (bf16[512,256]{1,0:T(8,128)(2,1)S(1)}, bf16[512,256]{1,0:T(8,128)(2,1)S(1)}, bf16[512,256]{1,0:T(8,128)(2,1)S(1)}) custom-call(s32[16]{0:T(128)} %pages_ref.1, s32[496]{0:T(512)} %length_ref.1, bf16[512,256]{1,0:T(8,128)(2,1)} %bitcast.12, s32[1024,256]{1,0:T(8,128)} %q_words.1, s32[1024,256]{1,0:T(8,128)} %bitcast.11, ...), custom_call_target="tpu_custom_call" | custom-call | flops 4294967296 | bytes 4194304 | tf_op jit(solution)/shard_map/gather_project/pallas_call | solution.py:546
  125.0 0.0 copy-start
  125.1 0.0 copy-start.1
  125.1 0.0 copy-done.3
  125.1 0.0 copy-done.4
  125.1 0.0 copy-done.2
  125.1 28.5 %conditional.1 = (bf16[512,256]{1,0:T(8,128)(2,1)S(1)}) conditional(s32[]{:T(128)} %convert_element_type.3, (s32[16]{0:T(128)S(1)}, s32[496,16]{0,1:T(8,128)S(1)}, s32[496]{0:T(512)S(1)}, bf16[512,256]{1,0:T(8,128)(2,1)S(1)}, bf16[512,256]{1,0:T(8,128)(2,1)S(1)}, /*index=5*/bf16[512,256]{1,0:T(8,128)(2,1)S(1)}, ...), branch_computations={%region_0.2_spmd, %region_2.3_spmd} | conditional | flops 9744 | bytes 206544 | solution.py:615
  125.1 0.1 copy.20
  125.2 0.1 reduce
  125.4 0.1 pad_add_fusion.1
  125.5 0.1 pad_add_fusion
  125.5 0.1 copy.21
  125.7 0.1 reshape.29.table_ref
  125.8 0.1 copy.22.length_ref
  126.0 27.4 %decode.1 = bf16[512,256]{1,0:T(8,128)(2,1)S(1)} custom-call(s32[8192]{0:T(1024)S(1)} %reshape.29.table_ref, s32[512,1]{1,0:T(8,128)S(1)} %copy.22.length_ref, bf16[512,256]{1,0:T(8,128)(2,1)S(1)} %get-tuple-element.31.q_ref, bf16[512,256]{1,0:T(8,128)(2,1)S(1)} %get-tuple-element.32.kv_ref, bf16[512,256]{1,0:T(8,128)(2,1)S(1)} %get-tuple-element.33.fresh_ref, ...), custom_call_target="tpu_custom_call" | custom-call | tf_op jit(solution)/shard_map/cond/branch_0_fun/decode/pallas_call | solution.py:603
  153.6 0.0 copy-done
  153.6 0.0 copy-done.1
  153.6 65.9 %project_scatter.1 = bf16[512,256]{1,0:T(8,128)(2,1)S(1)} custom-call(bf16[512,256]{1,0:T(8,128)(2,1)S(1)} %get-tuple-element.58.att_ref, s32[32,8192]{1,0:T(8,128)S(1)} %copy-done, bf16[2,8192]{1,0:T(2,128)(2,1)S(1)} %copy-done.1), custom_call_target="tpu_custom_call" | custom-call | flops 2147483648 | bytes 4194304 | tf_op jit(solution)/shard_map/project_scatter/pallas_call | solution.py:617
  219.5 0.7 copy.26
  (3 shorter events, 0.1 us)
Async XLA Ops:
  0.0 125.1 %copy-start.3 = (s32[16]{0:T(128)S(1)}, s32[16]{0:T(128)}, u32[]{:S(2)}) copy-start(s32[16]{0:T(128)} %pages_ref.1) | copy-start | bytes 196
  0.0 125.1 %copy-start.4 = (s32[496]{0:T(512)S(1)}, s32[496]{0:T(512)}, u32[]{:S(2)}) copy-start(s32[496]{0:T(512)} %length_ref.1) | copy-start | bytes 5956
  0.0 125.1 %copy-start.2 = (s32[496,16]{0,1:T(8,128)S(1)}, s32[496,16]{0,1:T(8,128)}, u32[]{:S(2)}) copy-start(s32[496,16]{0,1:T(8,128)} %param.26) | copy-start | bytes 95236
  125.0 28.5 %copy-start = (s32[32,8192]{1,0:T(8,128)S(1)}, s32[32,8192]{1,0:T(8,128)}, u32[]{:S(2)}) copy-start(s32[32,8192]{1,0:T(8,128)} %ow.1) | copy-start | bytes 3145732
  125.1 28.5 %copy-start.1 = (bf16[2,8192]{1,0:T(2,128)(2,1)S(1)}, bf16[2,8192]{1,0:T(2,128)(2,1)}, u32[]{:S(2)}) copy-start(bf16[2,8192]{1,0:T(2,128)(2,1)} %scale_ref.1) | copy-start | bytes 98308
